TPU v7x, 128 devices: a whole 4x4x4 slice. The times are simulated.
128 devices in a mesh: fsdp: 32 (over y_lo, z, x), rep: 4 (over y_hi, core).
Axes of the slice: x: 4, y: 4 (y_hi: 2, y_lo: 2; y = y_hi * 2 + y_lo), z: 4, core: 2. Of those that a mesh axis runs over, the one named last changes fastest.
Arguments:
- video_in: bfloat16 [128, 196, 1024], P(('fsdp', 'rep')), may hold values from -6 to 6
- audio_in: bfloat16 [128, 128, 1024], P(('fsdp', 'rep')), may hold values from -6 to 6
- bottle_in: bfloat16 [128, 8, 1024], P(('fsdp', 'rep')), may hold values from -6 to 6
- video_gain: float32 [1024], replicated, may hold values from 0.5 to 8
- audio_gain: float32 [1024], replicated, may hold values from 0.5 to 8
- video_qkv: bfloat16 [1024, 3072], P('fsdp'), may hold values from -0.18 to 0.18
- video_out: bfloat16 [1024, 1024], P('fsdp'), may hold values from -0.1875 to 0.1875
- audio_qkv: bfloat16 [1024, 3072], P('fsdp'), may hold values from -0.18 to 0.18
- audio_out: bfloat16 [1024, 1024], P('fsdp'), may hold values from -0.1875 to 0.1875
- grad_video: bfloat16 [128, 196, 1024], P(('fsdp', 'rep')), may hold values from -6 to 6
- grad_audio: bfloat16 [128, 128, 1024], P(('fsdp', 'rep')), may hold values from -6 to 6
- grad_bottle: bfloat16 [128, 8, 1024], P(('fsdp', 'rep')), may hold values from -6 to 6
Outputs:
- dvideo_in: bfloat16 [128, 196, 1024], P(('fsdp', 'rep'))
- daudio_in: bfloat16 [128, 128, 1024], P(('fsdp', 'rep'))
- dbottle_in: bfloat16 [128, 8, 1024], P(('fsdp', 'rep'))
- video_qkv_grad: float32 [1024, 3072], P('fsdp')
- video_out_grad: float32 [1024, 1024], P('fsdp')
- audio_qkv_grad: float32 [1024, 3072], P('fsdp')
- audio_out_grad: float32 [1024, 1024], P('fsdp')
- video_gain_grad: float32 [1024], replicated
- audio_gain_grad: float32 [1024], replicated
All inputs are finite; a program needn't handle non-finite values.
Results may differ from a plain program's by a relative error of at most 0.025.
Values may be sent and summed in bfloat16 or wider, within the bound.
No kernel may reach another device: no remote copies, remote signals or barrier semaphores. Data moves between devices by JAX's collectives and lax.ppermute only.
A program may use at most 128 MiB of HBM per device.

v0:
```python
import functools

import jax
import jax.numpy as jnp
from jax import lax
from jax.experimental import pallas as pl
from jax.experimental.pallas import tpu as pltpu
from jax.sharding import Mesh
from jax.sharding import PartitionSpec as P

HEAD = 64
FSDP = ("fsdp_0", "fsdp_1", "fsdp_2")
FSDP_REP = ("fsdp_0", "fsdp_1", "fsdp_2", "rep_0", "rep_1")

f32 = jnp.float32
bf16 = jnp.bfloat16

RING = 4


def place_of(y, z, x, c):
    return (((y % 2) * RING + z) * RING + x) * 4 + (y // 2) * 2 + c


def pairs(move):
    out = []
    for y in range(RING):
        for z in range(RING):
            for x in range(RING):
                for c in range(2):
                    ny, nz, nx, nc = move(y, z, x, c)
                    out.append((place_of(y, z, x, c), place_of(ny % RING, nz % RING, nx % RING, nc)))
    return out


def send(value, move):
    return lax.ppermute(value, FSDP_REP, pairs(move))


def along_y(step):
    return lambda y, z, x, c: (y + step, z, x, c)


def along_last(step):
    return lambda y, z, x, c: (y, z + step * c, x + step * (1 - c), c)


def along_mid(step):
    return lambda y, z, x, c: (y, z + step * (1 - c), x + step * c, c)


def to_partner(y, z, x, c):
    return (y, z, x, 1 - c)


MID = ((0, 0), (0, 1), (-1, 0), (-1, 1), (1, 0), (1, 1), (2, 0), (2, 1))
LAST = (0, -1, 1, 2)


def coordinates():
    return jnp.stack([lax.axis_index(name) for name in ("fsdp_1", "fsdp_2", "rep_1", "fsdp_0")]).astype(jnp.int32)


def block_row(where, block):
    z, x, c = where[0], where[1], where[2]
    last = LAST[block // 8]
    mid, half = MID[block % 8]
    zz = (z + mid * (1 - c) + last * c) & (RING - 1)
    xx = (x + last * (1 - c) + mid * c) & (RING - 1)
    return pl.multiple_of(half * 512 + zz * 128 + xx * 32, 32)


def in_vmem(n):
    return [pl.BlockSpec(memory_space=pltpu.VMEM)] * n


def in_smem():
    return pl.BlockSpec(memory_space=pltpu.SMEM)


def dot_nn(a, b):
    return lax.dot_general(a, b, (((1,), (0,)), ((), ())), preferred_element_type=f32)


def dot_nt(a, b):
    return lax.dot_general(a, b, (((1,), (1,)), ((), ())), preferred_element_type=f32)


def dot_tn(a, b):
    return lax.dot_general(a, b, (((0,), (0,)), ((), ())), preferred_element_type=f32)


def local_body(length, placed, where, own, peer, gain, *refs):
    size = own.shape[1]
    n_weights = 2 if placed else 20
    weights, refs = refs[:n_weights], refs[n_weights:]
    grads, refs = refs[:7], refs[7:]
    dh, gain_part, refs = refs[0], refs[1], refs[2:]
    if placed:
        before, weights = weights[1], weights[:1]
    hidden, hidden_t, dyb, qkv, datt, att, dqkv, gqkv, gout, wqkv, wout = refs

    if placed:
        (full,) = weights
        base = pl.multiple_of(where[2] * 512, 512)

        def w_qkv(n):
            top = pl.multiple_of((n // 5) * 1024, 1024)
            return full[pl.ds(top, 1024), pl.ds(pl.multiple_of((n % 5) * 256, 256), 256)]

        def w_out(half):
            return full[pl.ds(1024 + base, 512), 256 + 512 * half : 768 + 512 * half]
    else:
        for n, ref in enumerate(weights):
            for k in range(ref.shape[0]):
                at = block_row(where, PIECE_BLOCKS[n][k])
                wqkv[pl.ds(at, 32), :] = ref[k, :, :1536]
                wout[pl.ds(at, 32), :] = ref[k, :, 1536:]

        def w_qkv(n):
            return wqkv[:, pl.ds(pl.multiple_of(n * 256, 256), 256)]

        def w_out(half):
            return wout[512 * half : 512 * half + 512, :]

    for b, pair in enumerate((own, peer)):
        z = pair[0].astype(f32)
        inverse = lax.rsqrt(jnp.mean(z * z, axis=1, keepdims=True) + 1e-06)
        hidden[b * size : (b + 1) * size, :] = (z * inverse * gain[...]).astype(bf16)
        dyb[b * size : (b + 1) * size, :] = pair[1]
    hidden_t[...] = hidden[...].T

    @pl.loop(0, 6)
    def _(n):
        at = pl.multiple_of(n * 256, 256)
        qkv[:, pl.ds(at, 256)] = dot_nn(hidden[...], w_qkv(n)).astype(bf16)

    datt[...] = (dot_nt(dyb[:, :512], w_out(0)) + dot_nt(dyb[:, 512:], w_out(1))).astype(bf16)

    scale = HEAD ** (-0.5)
    lane = lax.broadcasted_iota(jnp.int32, (size, 128), 1)
    key_at = lax.broadcasted_iota(jnp.int32, (size, size), 1)
    zero = jnp.zeros((), bf16)

    @pl.loop(0, 8)
    def _(n):
        r = pl.ds(pl.multiple_of((n // 4) * size, 16), size)
        at = pl.multiple_of((n % 4) * 128, 128)
        query = qkv[r, pl.ds(at, 128)]
        keyed = qkv[r, pl.ds(at + 512, 128)]
        valued = qkv[r, pl.ds(at + 1024, 128)]
        dout = datt[r, pl.ds(at, 128)]
        sums = [None] * 4
        for head in range(2):
            mine = (lane < HEAD) if head == 0 else (lane >= HEAD)
            q = jnp.where(mine, query, zero)
            k = jnp.where(mine, keyed, zero)
            v = jnp.where(mine, valued, zero)
            d = jnp.where(mine, dout, zero)
            score = dot_nt(q, keyed) * scale
            score = jnp.where(key_at < length, score, -1e30)
            top = jnp.max(score, axis=1, keepdims=True)
            grown = jnp.exp(score - top)
            probs = grown * (1.0 / jnp.sum(grown, axis=1, keepdims=True))
            pb = probs.astype(bf16)
            dprob = dot_nt(d, valued)
            inner = jnp.sum(probs * dprob, axis=1, keepdims=True)
            dsb = (probs * (dprob - inner) * scale).astype(bf16)
            parts = (dot_nn(pb, v), dot_nn(dsb, k), dot_tn(dsb, q), dot_tn(pb, d))
            sums = [p if t is None else t + p for t, p in zip(sums, parts)]
        att[r, pl.ds(at, 128)] = sums[0].astype(bf16)
        dqkv[r, pl.ds(at, 128)] = sums[1].astype(bf16)
        dqkv[r, pl.ds(at + 512, 128)] = sums[2].astype(bf16)
        dqkv[r, pl.ds(at + 1024, 128)] = sums[3].astype(bf16)

    att_t = att[...].T
    for half in range(2):
        gout[512 * half : 512 * half + 512, :] = dot_nn(
            att_t, dyb[:, 512 * half : 512 * half + 512]
        ).astype(bf16)

    @pl.loop(0, 6)
    def _(n):
        at = pl.multiple_of(n * 256, 256)
        gqkv[:, pl.ds(at, 256)] = dot_nn(hidden_t[...], dqkv[:, pl.ds(at, 256)]).astype(bf16)

    for n, ref in enumerate(grads):
        for k, block in enumerate(GRAD_BLOCKS[n]):
            at = block_row(where, block)
            ref[32 * k : 32 * k + 32, :1536] = gqkv[pl.ds(at, 32), :]
            ref[32 * k : 32 * k + 32, 1536:] = gout[pl.ds(at, 32), :]

    part = jnp.zeros((1, 1024), f32)
    for b, pair in enumerate((own, peer)):
        total = dot_nt(dqkv[b * size : (b + 1) * size, :256], w_qkv(0))
        for k in range(1, 6):
            total = total + dot_nt(dqkv[b * size : (b + 1) * size, k * 256 : k * 256 + 256], w_qkv(k))
        dh[b] = total
        z = pair[0].astype(f32)
        normed = z * lax.rsqrt(jnp.mean(z * z, axis=1, keepdims=True) + 1e-06)
        part = part + jnp.sum(total * normed, axis=0, keepdims=True)
    if placed:
        both = jnp.concatenate([before[...], part], 1)
        gain_part[...] = both
        for ref in grads[5:]:
            ref[128:144, :] = in_pieces(both)
    else:
        gain_part[...] = part


def in_pieces(value):
    first = value.astype(bf16).astype(f32)
    second = (value - first).astype(bf16).astype(f32)
    third = value - first - second
    row = lax.broadcasted_iota(jnp.int32, (16, value.shape[1]), 0)
    out = jnp.where(row == 0, first, jnp.where(row == 1, second, third))
    return jnp.where(row < 3, out, 0.0).astype(bf16)


def from_pieces(rows):
    rows = rows.astype(f32)
    return (rows[0:1] + rows[1:2]) + rows[2:3]


PIECE_BLOCKS = []
for start in (0, 8, 16):
    PIECE_BLOCKS += [(start, start + 1), (start + 2, start + 3), (start + 4, start + 5), (start + 6,), (start + 7,)]
PIECE_BLOCKS += [(24, 25), (26, 27), (28, 29), (30,), (31,)]
GRAD_BLOCKS = [tuple(range(8))]
for start in (8, 16, 24):
    GRAD_BLOCKS += [tuple(range(start, start + 4)), tuple(range(start + 4, start + 8))]


def local_compute(length, placed, where, own, peer, gain, weights):
    size = own.shape[1]
    total = 2 * size
    return pl.pallas_call(
        lambda *refs: local_body(length, placed, *refs),
        in_specs=[in_smem()] + in_vmem(3 + len(weights)),
        out_specs=in_vmem(9),
        out_shape=[jax.ShapeDtypeStruct((256, 2048), bf16)]
        + [jax.ShapeDtypeStruct((128, 2048), bf16)] * 4
        + [jax.ShapeDtypeStruct((144 if placed else 128, 2048), bf16)] * 2
        + [
            jax.ShapeDtypeStruct((2, size, 1024), f32),
            jax.ShapeDtypeStruct((1, 2048 if placed else 1024), f32),
        ],
        scratch_shapes=[
            pltpu.VMEM((total, 1024), bf16),
            pltpu.VMEM((1024, total), bf16),
            pltpu.VMEM((total, 1024), bf16),
            pltpu.VMEM((total, 1536), bf16),
            pltpu.VMEM((total, 512), bf16),
            pltpu.VMEM((total, 512), bf16),
            pltpu.VMEM((total, 1536), bf16),
            pltpu.VMEM((1024, 1536), bf16),
            pltpu.VMEM((1024, 512), bf16),
            pltpu.VMEM((16 if placed else 1024, 1536), bf16),
            pltpu.VMEM((16 if placed else 1024, 512), bf16),
        ],
        name="local_placed" if placed else "local_pieces",
    )(where, own, peer, gain.reshape(1, 1024), *weights)


def my_columns(qkv_shard):
    c = lax.axis_index("rep_1")
    halves = qkv_shard.reshape(32, 3, 2, 512)
    return jnp.where(c == 0, halves[:, :, 0], halves[:, :, 1]).reshape(32, 1536)


def gather_by_calls(qkv_shard, out_shard):
    high = lax.axis_index("rep_0")
    shard = jnp.concatenate([my_columns(qkv_shard), out_shard], 1)
    shard = jnp.where(high == 0, shard[:, :1280], shard[:, 1280:])
    return lax.all_gather(shard, ("rep_0",) + FSDP, axis=0, tiled=True)


def gather_by_rings(qkv_shard, out_shard):
    low = lax.axis_index("fsdp_0")
    c = lax.axis_index("rep_1")
    shard = jnp.concatenate([my_columns(qkv_shard), out_shard], 1)
    top = send(shard[:16], along_y(1))
    bottom = send(shard[16:], along_y(-1))
    other = jnp.concatenate([top, bottom], 0)
    first = jnp.where(low == 0, shard[:, :1536], other[:, :1536])
    second = jnp.where(low == 0, other[:, :1536], shard[:, :1536])
    outw = jnp.where(low == c, shard[:, 1536:], other[:, 1536:])
    block = jnp.stack(
        [
            jnp.concatenate([first, outw[:, :512]], 1),
            jnp.concatenate([second, outw[:, 512:]], 1),
        ]
    )
    left = send(block, along_mid(1))
    right = send(block, along_mid(-1))
    far_a = send(left[:1], along_mid(1))
    far_b = send(right[1:], along_mid(-1))
    own = [block, left, right, far_a, far_b]
    from_left = [send(piece, along_last(1)) for piece in own]
    from_right = [send(piece, along_last(-1)) for piece in own]
    across = [send(piece, along_last(1)) for piece in from_left[:2]]
    across += [send(piece, along_last(-1)) for piece in from_right[2:]]
    return own + from_left + from_right + across


def add(*terms):
    total = terms[0].astype(f32)
    for term in terms[1:]:
        total = total + term.astype(f32)
    return total


def in_one_kernel(body, shapes, *args, scalars=None):
    specs = in_vmem(len(args))
    if scalars is not None:
        specs = [in_smem()] + specs
        args = (scalars,) + args
    return pl.pallas_call(
        body,
        in_specs=specs,
        out_specs=in_vmem(len(shapes)),
        out_shape=[jax.ShapeDtypeStruct(shape, dtype) for shape, dtype in shapes],
    )(*args)


def fold_far(right, left, up, down, right_out, left_out):
    right_out[:128, :] = add(right[...], up[:128, :]).astype(bf16)
    left_out[...] = add(left[...], down[:128, :]).astype(bf16)
    if right_out.shape[0] > 128:
        right_out[128:, :] = up[128:, :]


def first_steps(grads):
    own, left_a, left_b, right_a, right_b, far_a, far_b = grads
    up_far = send(far_a, along_last(1))
    down_far = send(far_b, along_last(-1))
    up_b = send(right_b, along_last(1))
    down_a = send(left_a, along_last(-1))
    return own, left_b, right_a, up_far, down_far, up_b, down_a


def second_steps(parts):
    own, left_b, right_a, up_far, down_far, up_b, down_a = parts
    right, left = in_one_kernel(
        fold_far, [(up_far.shape, bf16), ((128, 2048), bf16)], right_a, left_b, up_far, down_far
    )
    up_a = send(right, along_last(1))
    down_b = send(left, along_last(-1))
    return own, up_a, up_b, down_a, down_b


def ring_sum(own, left, right, far):
    return (own + far) + (left + right)


def fold_last(v_own, v_up_a, v_up_b, v_down_a, v_down_b, own, up_a, up_b, down_a, down_b,
              gain, up_far, down_far, far_up, far_down, right, left, home, gain_out):
    parts = (
        (v_own, v_up_a, v_up_b, v_down_a, v_down_b),
        (own, up_a, up_b, down_a, down_b),
    )
    for s, (o, ua, ub, da, db) in enumerate(parts):
        for j in range(8):
            u, d, at = (ua, da, 32 * j) if j < 4 else (ub, db, 32 * j - 128)
            total = add(o[32 * j : 32 * j + 32, :], u[at : at + 32, :], d[at : at + 32, :])
            if j < 2:
                home[64 * s + 32 * j : 64 * s + 32 * j + 32, :] = total
            else:
                ref = (left, right, None)[(j - 2) // 2]
                if ref is None:
                    ref = far_up if j == 6 else far_down
                    ref[32 * s : 32 * s + 32, :] = total.astype(bf16)
                else:
                    row = 64 * s + 32 * (j % 2)
                    ref[row : row + 32, :] = total.astype(bf16)
    total = ring_sum(
        gain[...],
        from_pieces(up_far[128:144, :]),
        from_pieces(down_far[128:144, :]),
        from_pieces(up_a[128:144, :]),
    )
    gain_out[...] = total
    far_up[64:80, :] = in_pieces(total)
    far_down[64:80, :] = in_pieces(total)


def fold_mid_far(right, left, up, down, right_out, left_out):
    for s in range(2):
        a, b, c = 64 * s, 64 * s + 32, 64 * s + 64
        right_out[a:b, :] = add(right[a:b, :], up[32 * s : 32 * s + 32, :]).astype(bf16)
        right_out[b:c, :] = right[b:c, :]
        left_out[a:b, :] = left[a:b, :]
        left_out[b:c, :] = add(left[b:c, :], down[32 * s : 32 * s + 32, :]).astype(bf16)
    right_out[128:144, :] = up[64:80, :]


def fold_mid(where, home, gain, up, down, up_far, down_far, same, cross, gain_out):
    low = where[3]
    for s in range(2):
        first, second = (
            add(home[r, :], up[r, :], down[r, :]).astype(bf16)
            for r in (pl.ds(64 * s, 32), pl.ds(64 * s + 32, 32))
        )
        r = slice(32 * s, 32 * s + 32)
        flip = jnp.full((32, 1536), low, jnp.int32) == 1
        a, b = first[:, :1536].astype(f32), second[:, :1536].astype(f32)
        same[r, :1536] = jnp.where(flip, b, a).astype(bf16)
        cross[r, :1536] = jnp.where(flip, a, b).astype(bf16)
        for ref in (same, cross):
            ref[r, 1536:2048] = first[:, 1536:]
            ref[r, 2048:] = second[:, 1536:]
    total = ring_sum(
        gain[...],
        from_pieces(up_far[64:80, :]),
        from_pieces(down_far[64:80, :]),
        from_pieces(up[128:144, :]),
    )
    gain_out[...] = total
    for ref in (same, cross):
        ref[64:80, :2048] = in_pieces(total)
        ref[64:80, 2048:] = jnp.zeros((16, 512), bf16)


def fold_y(count, same, up, down, far, gain, out):
    total = add(same[:64, :], far[:64, :]) + add(up[:64, :], down[:64, :])
    out[:64, :] = total / count
    total = ring_sum(
        gain[...],
        from_pieces(up[64:80, :2048]),
        from_pieces(down[64:80, :2048]),
        from_pieces(far[64:80, :2048]),
    )
    out[64:72, :2048] = jnp.broadcast_to(total, (8, 2048))
    out[64:72, 2048:] = jnp.zeros((8, 512), f32)


def spread(count, where, mine, peer, v_qkv, v_out, a_qkv, a_out, gain_v, gain_a):
    c, low = where[2], where[3]
    for s, (qkv, out) in enumerate(((v_qkv, v_out), (a_qkv, a_out))):
        r = slice(32 * s, 32 * s + 32)
        for k in range(3):
            at = pl.multiple_of(1024 * k + 512 * c, 512)
            qkv[:, pl.ds(at, 512)] = mine[r, 512 * k : 512 * k + 512]
            at = pl.multiple_of(1024 * k + 512 * (1 - c), 512)
            qkv[:, pl.ds(at, 512)] = peer[r, 512 * k : 512 * k + 512]
        here = jnp.full((32, 1024), (low == c).astype(jnp.int32), jnp.int32) == 1
        out[...] = jnp.where(here, mine[r, 1536:], peer[r, 1536:])
    total = (mine[64:72, :2048] + peer[64:72, :2048]) / count
    gain_v[...] = total[0:1, :1024]
    gain_a[...] = total[0:1, 1024:]


def last_steps(video, audio, audio_parts, gain, where, count):
    audio_far = audio_parts[3:5]
    far_up, far_down, right, left, home, gain = in_one_kernel(
        fold_last,
        [((80, 2048), bf16)] * 2
        + [((128, 2048), bf16)] * 2
        + [((128, 2048), f32), ((1, 2048), f32)],
        *video,
        *audio,
        gain,
        *audio_far,
    )
    up_far = send(far_up, along_mid(1))
    down_far = send(far_down, along_mid(-1))
    right, left = in_one_kernel(
        fold_mid_far, [((144, 2048), bf16), ((128, 2048), bf16)], right, left, up_far, down_far
    )
    up = send(right, along_mid(1))
    down = send(left, along_mid(-1))
    same, cross, gain = in_one_kernel(
        fold_mid,
        [((80, 2560), bf16)] * 2 + [((1, 2048), f32)],
        home,
        gain,
        up,
        down,
        up_far,
        down_far,
        scalars=where,
    )
    far = send(same, along_y(2))
    up = send(cross, along_y(1))
    down = send(cross, along_y(-1))
    (total,) = in_one_kernel(
        functools.partial(fold_y, count), [((72, 2560), f32)], same, up, down, far, gain
    )
    peer = send(total, to_partner)
    return in_one_kernel(
        functools.partial(spread, count),
        [((32, 3072), f32), ((32, 1024), f32)] * 2 + [((1, 1024), f32)] * 2,
        total,
        peer,
        scalars=where,
    )


def clip_pair(tokens, bottle, d_tokens, d_bottle):
    half = (d_bottle.astype(f32) * 0.5).astype(bf16)
    pad = jnp.zeros((-(tokens.shape[0] + bottle.shape[0]) % 16, 1024), bf16)
    own = jnp.stack(
        [jnp.concatenate([tokens, bottle, pad], 0), jnp.concatenate([d_tokens, half, pad], 0)]
    )
    return own, send(own, to_partner)


def finish(own, gain, dh):
    dhidden = dh[0] + send(dh[1], to_partner)
    z = own[0].astype(f32)
    inverse = lax.rsqrt(jnp.mean(z * z, axis=1, keepdims=True) + 1e-06)
    normed = z * inverse
    dnorm = dhidden * gain
    d_out = own[1].astype(f32)
    d_z = d_out + inverse * (dnorm - normed * jnp.mean(dnorm * normed, axis=1, keepdims=True))
    return d_z


def per_device(
    video_in,
    audio_in,
    bottle_in,
    video_gain,
    audio_gain,
    video_qkv,
    video_out,
    audio_qkv,
    audio_out,
    grad_video,
    grad_audio,
    grad_bottle,
):
    count = float(video_in.shape[0] * lax.axis_size(FSDP_REP))
    where = coordinates()
    video_len = video_in.shape[1]
    audio_len = audio_in.shape[1]
    bottle_len = bottle_in.shape[1]
    aweights = gather_by_calls(audio_qkv, audio_out)
    vweights = gather_by_rings(video_qkv, video_out)
    vown, vpeer = clip_pair(video_in[0], bottle_in[0], grad_video[0], grad_bottle[0])
    aown, apeer = clip_pair(audio_in[0], bottle_in[0], grad_audio[0], grad_bottle[0])
    vpeer, apeer = lax.optimization_barrier((vpeer, apeer))
    *grads, dh_video, gain_v = local_compute(
        video_len + bottle_len, False, where, vown, vpeer, video_gain, vweights
    )
    video_parts = first_steps(grads)
    *grads, dh_audio, gain = local_compute(
        audio_len + bottle_len,
        True,
        where,
        aown,
        apeer,
        audio_gain,
        [aweights, gain_v],
    )
    audio_parts = first_steps(grads)
    video = second_steps(video_parts)
    audio = second_steps(audio_parts)
    (
        video_qkv_grad,
        video_out_grad,
        audio_qkv_grad,
        audio_out_grad,
        gain_v,
        gain_a,
    ) = last_steps(video, audio, audio_parts, gain, where, count)
    dz_video = finish(vown, video_gain, dh_video)
    dz_audio = finish(aown, audio_gain, dh_audio)
    video_end = video_len + bottle_len
    audio_end = audio_len + bottle_len
    dvideo_in = dz_video[None, :video_len].astype(bf16)
    daudio_in = dz_audio[None, :audio_len].astype(bf16)
    dbottle_in = dz_video[None, video_len:video_end] + dz_audio[None, audio_len:audio_end]
    dbottle_in = dbottle_in.astype(bf16)
    return (
        dvideo_in,
        daudio_in,
        dbottle_in,
        video_qkv_grad,
        video_out_grad,
        audio_qkv_grad,
        audio_out_grad,
        gain_v[0],
        gain_a[0],
    )


def solution(mesh):
    split = Mesh(
        mesh.devices.reshape(2, 4, 4, 2, 2), ("fsdp_0", "fsdp_1", "fsdp_2", "rep_0", "rep_1")
    )
    return jax.shard_map(
        per_device,
        mesh=split,
        in_specs=(
            P(FSDP_REP, None, None),
            P(FSDP_REP, None, None),
            P(FSDP_REP, None, None),
            P(),
            P(),
            P(FSDP, None),
            P(FSDP, None),
            P(FSDP, None),
            P(FSDP, None),
            P(FSDP_REP, None, None),
            P(FSDP_REP, None, None),
            P(FSDP_REP, None, None),
        ),
        out_specs=(
            P(FSDP_REP, None, None),
            P(FSDP_REP, None, None),
            P(FSDP_REP, None, None),
            P(FSDP, None),
            P(FSDP, None),
            P(FSDP, None),
            P(FSDP, None),
            P(),
            P(),
        ),
        check_vma=False,
    )
```

profile of v0, /device:TPU:1, one launch (start us, length us, event | category | flops | bytes accessed | tf_op | source)
XLA Modules:
  0.0 238.8 jit_solution(13229386474259686047)
XLA Ops:
  10.2 2.2 collective-permute-start.2
  15.7 2.1 collective-permute-done.3
  19.4 1.5 collective-permute-start.5
  20.9 1.6 collective-permute-start.8
  22.7 2.3 collective-permute-start
  25.0 3.5 %collective-permute-start.13 = (bf16[2,32,2048]{2,1,0:T(8,128)(2,1)S(1)}, bf16[2,32,2048]{2,1,0:T(8,128)(2,1)S(1)}, u32[]{:S(2)}, u32[]{:S(2)}) collective-permute-start(bf16[2,32,2048]{2,1,0:T(8,128)(2,1)S(1)} %pad_maximum_fusion.2.refs_4_), channel_id=1, source_target_pairs={{0,12},{1,49},{4,0},{5,53},{8,4},{9,57},{12,8},{13,61},{16,28},{17... | collective-permute-start | bytes 786440 | tf_op jit(solution)/shard_map/ppermute | solution.py:37
  28.6 1.5 collective-permute-done.8.refs_9_
  33.2 2.1 collective-permute-done.6.refs_7_
  35.3 1.4 collective-permute-done.7.refs_8_
  36.7 3.0 %collective-permute-start.14 = (bf16[2,32,2048]{2,1,0:T(8,128)(2,1)S(1)}, bf16[2,32,2048]{2,1,0:T(8,128)(2,1)S(1)}, u32[]{:S(2)}, u32[]{:S(2)}) collective-permute-start(bf16[2,32,2048]{2,1,0:T(8,128)(2,1)S(1)} %collective-permute-done.4.refs_5_), channel_id=1, source_target_pairs={{0,12},{1,49},{4,0},{5,53},{8,4},{9,57},{12,8},{13,61},{16,28},{17... | collective-permute-start | bytes 786440 | tf_op jit(solution)/shard_map/ppermute | solution.py:37
  39.7 1.4 collective-permute-start.18
  41.7 2.7 %collective-permute-done.14.refs_15_ = bf16[2,32,2048]{2,1,0:T(8,128)(2,1)S(1)} collective-permute-done((bf16[2,32,2048]{2,1,0:T(8,128)(2,1)S(1)}, bf16[2,32,2048]{2,1,0:T(8,128)(2,1)S(1)}, u32[]{:S(2)}, u32[]{:S(2)}) %collective-permute-start.14) | collective-permute-done | bytes 262176 | tf_op jit(solution)/shard_map/ppermute | solution.py:37
  44.4 3.4 %collective-permute-start.16 = (bf16[1,32,2048]{2,1,0:T(8,128)(2,1)S(1)}, bf16[1,32,2048]{2,1,0:T(8,128)(2,1)}, u32[]{:S(2)}, u32[]{:S(2)}) collective-permute-start(bf16[1,32,2048]{2,1,0:T(8,128)(2,1)S(1)} %collective-permute-done.6.refs_7_), channel_id=1, source_target_pairs={{0,12},{1,49},{4,0},{5,53},{8,4},{9,57},{12,8},{13,61},{16,28},{17... | collective-permute-start | bytes 393224 | tf_op jit(solution)/shard_map/ppermute | solution.py:37
  48.4 3.5 %collective-permute-start.17 = (bf16[1,32,2048]{2,1,0:T(8,128)(2,1)}, bf16[1,32,2048]{2,1,0:T(8,128)(2,1)}, u32[]{:S(2)}, u32[]{:S(2)}) collective-permute-start(bf16[1,32,2048]{2,1,0:T(8,128)(2,1)} %collective-permute-done.7.refs_8_), channel_id=1, source_target_pairs={{0,12},{1,49},{4,0},{5,53},{8,4},{9,57},{12,8},{13,61},{16,28},{17... | collective-permute-start | bytes 393224 | tf_op jit(solution)/shard_map/ppermute | solution.py:37
  52.0 2.7 %collective-permute-start.20 = (bf16[2,32,2048]{2,1,0:T(8,128)(2,1)S(1)}, bf16[2,32,2048]{2,1,0:T(8,128)(2,1)}, u32[]{:S(2)}, u32[]{:S(2)}) collective-permute-start(bf16[2,32,2048]{2,1,0:T(8,128)(2,1)S(1)} %collective-permute-done.15.refs_16_), channel_id=1, source_target_pairs={{0,12},{1,49},{4,0},{5,53},{8,4},{9,57},{12,8},{13,61},{16,28},{17... | collective-permute-start | bytes 786440 | tf_op jit(solution)/shard_map/ppermute | solution.py:37
  54.6 3.3 %collective-permute-start.21 = (bf16[1,32,2048]{2,1,0:T(8,128)(2,1)}, bf16[1,32,2048]{2,1,0:T(8,128)(2,1)}, u32[]{:S(2)}, u32[]{:S(2)}) collective-permute-start(bf16[1,32,2048]{2,1,0:T(8,128)(2,1)} %collective-permute-done.16.refs_17_), channel_id=1, source_target_pairs={{0,12},{1,49},{4,0},{5,53},{8,4},{9,57},{12,8},{13,61},{16,28},{17... | collective-permute-start | bytes 393224 | tf_op jit(solution)/shard_map/ppermute | solution.py:37
  58.9 2.2 collective-permute-done.12.refs_13_
  62.4 22.2 %local_pieces.1 = (bf16[256,2048]{1,0:T(8,128)(2,1)}, bf16[128,2048]{1,0:T(8,128)(2,1)}, bf16[128,2048]{1,0:T(8,128)(2,1)}, bf16[128,2048]{1,0:T(8,128)(2,1)}, b...) custom-call(s32[4]{0:T(128)} %pad_add_fusion.refs_0_.where, ...), custom_call_target="tpu_custom_call" | custom-call | tf_op jit(solution)/shard_map/local_pieces/pallas_call | solution.py:237
  84.8 20.8 %local_placed.1 = (bf16[256,2048]{1,0:T(8,128)(2,1)}, bf16[128,2048]{1,0:T(8,128)(2,1)}, bf16[128,2048]{1,0:T(8,128)(2,1)}, bf16[128,2048]{1,0:T(8,128)(2,1)}, b...) custom-call(s32[4]{0:T(128)} %pad_add_fusion.refs_0_.where, ...), custom_call_target="tpu_custom_call" | custom-call | tf_op jit(solution)/shard_map/local_placed/pallas_call | solution.py:237
  105.8 1.4 collective-permute-start.25
  108.5 1.4 collective-permute-start.32
  109.9 11.6 %collective-permute-done.25.up = bf16[128,2048]{1,0:T(8,128)(2,1)} collective-permute-done((bf16[128,2048]{1,0:T(8,128)(2,1)}, bf16[128,2048]{1,0:T(8,128)(2,1)}, u32[]{:S(2)}, u32[]{:S(2)}) %collective-permute-start.25) | collective-permute-done | bytes 524320 | tf_op jit(solution)/shard_map/ppermute | solution.py:37
  121.5 1.5 collective-permute-start.29
  123.0 2.6 %shard_map.187 = (bf16[128,2048]{1,0:T(8,128)(2,1)}, bf16[128,2048]{1,0:T(8,128)(2,1)}) custom-call(bf16[128,2048]{1,0:T(8,128)(2,1)} %get-tuple-element.56.right, bf16[128,2048]{1,0:T(8,128)(2,1)} %get-tuple-element.57.left, bf16[128,2048]{1,0:T(8,128)(2,1)} %collective-permute-done.25.up, bf16[128,2048]{1,0:T(8,128)(2,1)} %collective-permute-done.26.down), custom_call_target="tpu_custom_call" | custom-call | tf_op jit(solution)/shard_map/pallas_call | solution.py:318
  125.6 2.7 %collective-permute-start.30 = (bf16[128,2048]{1,0:T(8,128)(2,1)}, bf16[128,2048]{1,0:T(8,128)(2,1)}, u32[]{:S(2)}, u32[]{:S(2)}) collective-permute-start(bf16[128,2048]{1,0:T(8,128)(2,1)} %get-tuple-element.63), channel_id=1, source_target_pairs={{0,12},{1,49},{4,0},{5,53},{8,4},{9,57},{12,8},{13,61},{16,28},{17... | collective-permute-start | bytes 1572872 | tf_op jit(solution)/shard_map/ppermute | solution.py:37
  129.3 20.5 %collective-permute-start.23 = (f32[208,1024]{1,0:T(8,128)}, f32[208,1024]{1,0:T(8,128)S(1)}, u32[]{:S(2)}, u32[]{:S(2)}) collective-permute-start(f32[208,1024]{1,0:T(8,128)} %slice_bitcast_fusion), channel_id=1, source_target_pairs={{0,1},{1,0},{4,5},{5,4},{8,9},{9,8},{12,13},{13,12},{16,17},{17,16... | collective-permute-start | bytes 2555912 | tf_op jit(solution)/shard_map/ppermute | solution.py:37
  149.8 2.7 %shard_map.188 = (bf16[144,2048]{1,0:T(8,128)(2,1)}, bf16[128,2048]{1,0:T(8,128)(2,1)}) custom-call(bf16[128,2048]{1,0:T(8,128)(2,1)} %get-tuple-element.65.right, bf16[128,2048]{1,0:T(8,128)(2,1)} %get-tuple-element.66.left, bf16[144,2048]{1,0:T(8,128)(2,1)} %copy-done.6, bf16[144,2048]{1,0:T(8,128)(2,1)} %collective-permute-done.32.down.down_far), custom_call_target="tpu_custom_call" | custom-call | tf_op jit(solution)/shard_map/pallas_call | solution.py:318
  152.6 3.9 %collective-permute-start.35 = (bf16[128,2048]{1,0:T(8,128)(2,1)}, bf16[128,2048]{1,0:T(8,128)(2,1)}, u32[]{:S(2)}, u32[]{:S(2)}) collective-permute-start(bf16[128,2048]{1,0:T(8,128)(2,1)} %get-tuple-element.71), channel_id=1, source_target_pairs={{0,12},{1,49},{4,0},{5,53},{8,4},{9,57},{12,8},{13,61},{16,28},{17... | collective-permute-start | bytes 1572872 | tf_op jit(solution)/shard_map/ppermute | solution.py:37
  156.5 1.4 collective-permute-start.36
  159.6 10.0 %collective-permute-done.34.up_b = bf16[128,2048]{1,0:T(8,128)(2,1)} collective-permute-done((bf16[128,2048]{1,0:T(8,128)(2,1)}, bf16[128,2048]{1,0:T(8,128)(2,1)}, u32[]{:S(2)}, u32[]{:S(2)}) %collective-permute-start.34) | collective-permute-done | bytes 524320 | tf_op jit(solution)/shard_map/ppermute | solution.py:37
  170.0 5.1 %shard_map.189 = (bf16[80,2048]{1,0:T(8,128)(2,1)}, bf16[80,2048]{1,0:T(8,128)(2,1)}, bf16[128,2048]{1,0:T(8,128)(2,1)}, bf16[128,2048]{1,0:T(8,128)(2,1)}, f32[128,2048]{1,0:T(8,128)}, /*index=5*/f32[1,2048]{1,0:T(1,128)}) custom-call(bf16[256,2048]{1,0:T(8,128)(2,1)} %get-tuple-element.55.v_own, bf16[128,2048]{1,0:T(8,128)(2,1)} %collective-permute-done.27.v_up_a, ...), custom_call_target="tpu_custom_call" | custom-call | tf_op jit(solution)/shard_map/pallas_call | solution.py:318
  175.2 2.7 %collective-permute-start.38 = (bf16[80,2048]{1,0:T(8,128)(2,1)}, bf16[80,2048]{1,0:T(8,128)(2,1)}, u32[]{:S(2)}, u32[]{:S(2)}) collective-permute-start(bf16[80,2048]{1,0:T(8,128)(2,1)} %get-tuple-element.79), channel_id=1, source_target_pairs={{0,48},{1,13},{4,52},{5,1},{8,56},{9,5},{12,60},{13,9},{16,0},{17,... | collective-permute-start | bytes 983048 | tf_op jit(solution)/shard_map/ppermute | solution.py:37
  179.1 1.6 fusion.2
  180.7 2.1 collective-permute-done.37.up.up_far
  183.5 2.5 %shard_map.190 = (bf16[144,2048]{1,0:T(8,128)(2,1)}, bf16[128,2048]{1,0:T(8,128)(2,1)}) custom-call(bf16[128,2048]{1,0:T(8,128)(2,1)} %get-tuple-element.76.right, bf16[128,2048]{1,0:T(8,128)(2,1)} %get-tuple-element.77.left, bf16[80,2048]{1,0:T(8,128)(2,1)} %copy-done.9, bf16[80,2048]{1,0:T(8,128)(2,1)} %collective-permute-done.38.down.down_far), custom_call_target="tpu_custom_call" | custom-call | tf_op jit(solution)/shard_map/pallas_call | solution.py:318
  186.0 2.7 %collective-permute-start.40 = (bf16[128,2048]{1,0:T(8,128)(2,1)}, bf16[128,2048]{1,0:T(8,128)(2,1)S(1)}, u32[]{:S(2)}, u32[]{:S(2)}) collective-permute-start(bf16[128,2048]{1,0:T(8,128)(2,1)} %get-tuple-element.81), channel_id=1, source_target_pairs={{0,48},{1,13},{4,52},{5,1},{8,56},{9,5},{12,60},{13,9},{16,0},{17,... | collective-permute-start | bytes 1572872 | tf_op jit(solution)/shard_map/ppermute | solution.py:37
  188.7 1.9 slice_bitcast_fusion.1
  190.6 3.7 %collective-permute-start.24 = (f32[144,1024]{1,0:T(8,128)}, f32[144,1024]{1,0:T(8,128)}, u32[]{:S(2)}, u32[]{:S(2)}) collective-permute-start(f32[144,1024]{1,0:T(8,128)} %slice_bitcast_fusion.1), channel_id=1, source_target_pairs={{0,1},{1,0},{4,5},{5,4},{8,9},{9,8},{12,13},{13,12},{16,17},{17,16... | collective-permute-start | bytes 1769480 | tf_op jit(solution)/shard_map/ppermute | solution.py:37
  195.0 2.3 fusion.5
  198.3 3.0 %shard_map.191 = (bf16[80,2560]{1,0:T(8,128)(2,1)}, bf16[80,2560]{1,0:T(8,128)(2,1)}, f32[1,2048]{1,0:T(1,128)}) custom-call(s32[4]{0:T(128)} %pad_add_fusion.refs_0_.where, f32[128,2048]{1,0:T(8,128)} %get-tuple-element.74.home, f32[1,2048]{1,0:T(1,128)} %get-tuple-element.75.gain, bf16[144,2048]{1,0:T(8,128)(2,1)} %copy-done.17, ...), custom_call_target="tpu_custom_call" | custom-call | tf_op jit(solution)/shard_map/pallas_call | solution.py:318
  201.9 2.1 collective-permute-start.42
  205.6 1.4 fusion.10
  207.0 3.8 %collective-permute-done.41.up = bf16[80,2560]{1,0:T(8,128)(2,1)S(1)} collective-permute-done((bf16[80,2560]{1,0:T(8,128)(2,1)}, bf16[80,2560]{1,0:T(8,128)(2,1)S(1)}, u32[]{:S(2)}, u32[]{:S(2)}) %collective-permute-start.41) | collective-permute-done | bytes 409632 | tf_op jit(solution)/shard_map/ppermute | solution.py:37
  210.8 9.0 %collective-permute-done.43.far = bf16[80,2560]{1,0:T(8,128)(2,1)} collective-permute-done((bf16[80,2560]{1,0:T(8,128)(2,1)}, bf16[80,2560]{1,0:T(8,128)(2,1)}, u32[]{:S(2)}, u32[]{:S(2)}) %collective-permute-start.43) | collective-permute-done | bytes 409632 | tf_op jit(solution)/shard_map/ppermute | solution.py:37
  219.8 2.5 %shard_map.192.mine = f32[72,2560]{1,0:T(8,128)} custom-call(bf16[80,2560]{1,0:T(8,128)(2,1)} %get-tuple-element.82.same, bf16[80,2560]{1,0:T(8,128)(2,1)} %copy-done.23, bf16[80,2560]{1,0:T(8,128)(2,1)} %copy-done.24, bf16[80,2560]{1,0:T(8,128)(2,1)} %collective-permute-done.43.far, f32[1,2048]{1,0:T(1,128)} %get-tuple-element.84.gain), custom_call_target="tpu_custom_call" | custom-call | tf_op jit(solution)/shard_map/pallas_call | solution.py:318
  222.2 3.8 %collective-permute-start.44 = (f32[72,2560]{1,0:T(8,128)}, f32[72,2560]{1,0:T(8,128)S(1)}, u32[]{:S(2)}, u32[]{:S(2)}) collective-permute-start(f32[72,2560]{1,0:T(8,128)} %shard_map.192.mine), channel_id=1, source_target_pairs={{0,1},{1,0},{4,5},{5,4},{8,9},{9,8},{12,13},{13,12},{16,17},{17,16... | collective-permute-start | bytes 2211848 | tf_op jit(solution)/shard_map/ppermute | solution.py:37
  226.1 1.3 fusion.13
  229.6 2.4 shard_map.193
  (184 shorter events, 27.3 us)
Async XLA Ops:
  7.2 77.6 %all-gather.2.cloned.1.call-start = ((), (), s32[]{:S(2)}) async-start(), calls=%async_computation | async-start | bytes 5324800 | tf_op jit(solution)/shard_map/all_gather | solution.py:275
  10.2 5.5 %collective-permute-start.2 = (bf16[16,2560]{1,0:T(8,128)(2,1)S(1)}, bf16[16,2560]{1,0:T(8,128)(2,1)S(1)}, u32[]{:S(2)}, u32[]{:S(2)}) collective-permute-start(bf16[16,2560]{1,0:T(8,128)(2,1)S(1)} %get-tuple-element.98), channel_id=1, source_target_pairs={{0,64},{1,65},{4,68},{5,69},{8,72},{9,73},{12,76},{13,77},{16,80},... | collective-permute-start | bytes 245768 | tf_op jit(solution)/shard_map/ppermute | solution.py:37
  12.5 145.5 %copy-start.39 = (bf16[144]{0:T(256)(128)(2,1)}, bf16[144]{0:T(256)(128)(2,1)S(1)}, u32[]{:S(2)}) copy-start(bf16[144]{0:T(256)(128)(2,1)S(1)} %pad.15.clone) | copy-start | bytes 868
  12.8 26.9 %collective-permute-start.1 = (bf16[2,144,1024]{2,1,0:T(8,128)(2,1)S(1)}, bf16[2,144,1024]{2,1,0:T(8,128)(2,1)}, u32[]{:S(2)}, u32[]{:S(2)}) collective-permute-start(bf16[2,144,1024]{2,1,0:T(8,128)(2,1)S(1)} %pad_maximum_fusion.1.refs_1_), channel_id=1, source_target_pairs={{0,1},{1,0},{4,5},{5,4},{8,9},{9,8},{12,13},{13,12},{16,17},{17,16... | collective-permute-start | bytes 1769480 | tf_op jit(solution)/shard_map/ppermute | solution.py:37
  13.8 3.9 %collective-permute-start.3 = (bf16[16,2560]{1,0:T(8,128)(2,1)S(1)}, bf16[16,2560]{1,0:T(8,128)(2,1)S(1)}, u32[]{:S(2)}, u32[]{:S(2)}) collective-permute-start(bf16[16,2560]{1,0:T(8,128)(2,1)S(1)} %get-tuple-element.97), channel_id=1, source_target_pairs={{0,66},{1,67},{4,70},{5,71},{8,74},{9,75},{12,78},{13,79},{16,82},... | collective-permute-start | bytes 245768 | tf_op jit(solution)/shard_map/ppermute | solution.py:37
  15.2 143.5 %copy-start.41 = (bf16[208]{0:T(256)(128)(2,1)}, bf16[208]{0:T(256)(128)(2,1)S(1)}, u32[]{:S(2)}) copy-start(bf16[208]{0:T(256)(128)(2,1)S(1)} %pad.27.clone) | copy-start | bytes 1252
  17.9 7.1 %collective-permute-start.4 = (bf16[2,32,2048]{2,1,0:T(8,128)(2,1)S(1)}, bf16[2,32,2048]{2,1,0:T(8,128)(2,1)S(1)}, u32[]{:S(2)}, u32[]{:S(2)}) collective-permute-start(bf16[2,32,2048]{2,1,0:T(8,128)(2,1)S(1)} %pad_maximum_fusion.2.refs_4_), channel_id=1, source_target_pairs={{0,16},{1,5},{4,20},{5,9},{8,24},{9,13},{12,28},{13,1},{16,32},{17... | collective-permute-start | bytes 786440 | tf_op jit(solution)/shard_map/ppermute | solution.py:37
  19.4 9.0 %collective-permute-start.5 = (bf16[2,32,2048]{2,1,0:T(8,128)(2,1)S(1)}, bf16[2,32,2048]{2,1,0:T(8,128)(2,1)S(1)}, u32[]{:S(2)}, u32[]{:S(2)}) collective-permute-start(bf16[2,32,2048]{2,1,0:T(8,128)(2,1)S(1)} %pad_maximum_fusion.2.refs_4_), channel_id=1, source_target_pairs={{0,48},{1,13},{4,52},{5,1},{8,56},{9,5},{12,60},{13,9},{16,0},{17,... | collective-permute-start | bytes 786440 | tf_op jit(solution)/shard_map/ppermute | solution.py:37
  20.9 9.1 %collective-permute-start.8 = (bf16[2,32,2048]{2,1,0:T(8,128)(2,1)S(1)}, bf16[2,32,2048]{2,1,0:T(8,128)(2,1)S(1)}, u32[]{:S(2)}, u32[]{:S(2)}) collective-permute-start(bf16[2,32,2048]{2,1,0:T(8,128)(2,1)S(1)} %pad_maximum_fusion.2.refs_4_), channel_id=1, source_target_pairs={{0,4},{1,17},{4,8},{5,21},{8,12},{9,25},{12,0},{13,29},{16,20},{17... | collective-permute-start | bytes 786440 | tf_op jit(solution)/shard_map/ppermute | solution.py:37
  22.7 35.3 %collective-permute-start = (bf16[2,208,1024]{2,1,0:T(8,128)(2,1)S(1)}, bf16[2,208,1024]{2,1,0:T(8,128)(2,1)S(1)}, u32[]{:S(2)}, u32[]{:S(2)}) collective-permute-start(bf16[2,208,1024]{2,1,0:T(8,128)(2,1)S(1)} %pad_maximum_fusion.refs_1_), channel_id=1, source_target_pairs={{0,1},{1,0},{4,5},{5,4},{8,9},{9,8},{12,13},{13,12},{16,17},{17,16... | collective-permute-start | bytes 2555912 | tf_op jit(solution)/shard_map/ppermute | solution.py:37
  25.0 7.1 %collective-permute-start.13 = (bf16[2,32,2048]{2,1,0:T(8,128)(2,1)S(1)}, bf16[2,32,2048]{2,1,0:T(8,128)(2,1)S(1)}, u32[]{:S(2)}, u32[]{:S(2)}) collective-permute-start(bf16[2,32,2048]{2,1,0:T(8,128)(2,1)S(1)} %pad_maximum_fusion.2.refs_4_), channel_id=1, source_target_pairs={{0,12},{1,49},{4,0},{5,53},{8,4},{9,57},{12,8},{13,61},{16,28},{17... | collective-permute-start | bytes 786440 | tf_op jit(solution)/shard_map/ppermute | solution.py:37
  28.5 11.3 %collective-permute-start.9 = (bf16[2,32,2048]{2,1,0:T(8,128)(2,1)S(1)}, bf16[2,32,2048]{2,1,0:T(8,128)(2,1)}, u32[]{:S(2)}, u32[]{:S(2)}) collective-permute-start(bf16[2,32,2048]{2,1,0:T(8,128)(2,1)S(1)} %collective-permute-done.4.refs_5_), channel_id=1, source_target_pairs={{0,4},{1,17},{4,8},{5,21},{8,12},{9,25},{12,0},{13,29},{16,20},{17... | collective-permute-start | bytes 786440 | tf_op jit(solution)/shard_map/ppermute | solution.py:37
  30.1 5.2 %collective-permute-start.6 = (bf16[1,32,2048]{2,1,0:T(8,128)(2,1)S(1)}, bf16[1,32,2048]{2,1,0:T(8,128)(2,1)S(1)}, u32[]{:S(2)}, u32[]{:S(2)}) collective-permute-start(bf16[1,32,2048]{2,1,0:T(8,128)(2,1)S(1)} %slice.99), channel_id=1, source_target_pairs={{0,16},{1,5},{4,20},{5,9},{8,24},{9,13},{12,28},{13,1},{16,32},{17... | collective-permute-start | bytes 393224 | tf_op jit(solution)/shard_map/ppermute | solution.py:37
  32.0 4.7 %collective-permute-start.7 = (bf16[1,32,2048]{2,1,0:T(8,128)(2,1)S(1)}, bf16[1,32,2048]{2,1,0:T(8,128)(2,1)}, u32[]{:S(2)}, u32[]{:S(2)}) collective-permute-start(bf16[1,32,2048]{2,1,0:T(8,128)(2,1)S(1)} %slice.100), channel_id=1, source_target_pairs={{0,48},{1,13},{4,52},{5,1},{8,56},{9,5},{12,60},{13,9},{16,0},{17,... | collective-permute-start | bytes 393224 | tf_op jit(solution)/shard_map/ppermute | solution.py:37
  35.3 6.4 %collective-permute-start.10 = (bf16[2,32,2048]{2,1,0:T(8,128)(2,1)S(1)}, bf16[2,32,2048]{2,1,0:T(8,128)(2,1)S(1)}, u32[]{:S(2)}, u32[]{:S(2)}) collective-permute-start(bf16[2,32,2048]{2,1,0:T(8,128)(2,1)S(1)} %collective-permute-done.5.refs_6_), channel_id=1, source_target_pairs={{0,4},{1,17},{4,8},{5,21},{8,12},{9,25},{12,0},{13,29},{16,20},{17... | collective-permute-start | bytes 786440 | tf_op jit(solution)/shard_map/ppermute | solution.py:37
  36.7 7.7 %collective-permute-start.14 = (bf16[2,32,2048]{2,1,0:T(8,128)(2,1)S(1)}, bf16[2,32,2048]{2,1,0:T(8,128)(2,1)S(1)}, u32[]{:S(2)}, u32[]{:S(2)}) collective-permute-start(bf16[2,32,2048]{2,1,0:T(8,128)(2,1)S(1)} %collective-permute-done.4.refs_5_), channel_id=1, source_target_pairs={{0,12},{1,49},{4,0},{5,53},{8,4},{9,57},{12,8},{13,61},{16,28},{17... | collective-permute-start | bytes 786440 | tf_op jit(solution)/shard_map/ppermute | solution.py:37
  39.7 8.7 %collective-permute-start.15 = (bf16[2,32,2048]{2,1,0:T(8,128)(2,1)S(1)}, bf16[2,32,2048]{2,1,0:T(8,128)(2,1)S(1)}, u32[]{:S(2)}, u32[]{:S(2)}) collective-permute-start(bf16[2,32,2048]{2,1,0:T(8,128)(2,1)S(1)} %collective-permute-done.5.refs_6_), channel_id=1, source_target_pairs={{0,12},{1,49},{4,0},{5,53},{8,4},{9,57},{12,8},{13,61},{16,28},{17... | collective-permute-start | bytes 786440 | tf_op jit(solution)/shard_map/ppermute | solution.py:37
  39.7 12.2 %collective-permute-start.18 = (bf16[2,32,2048]{2,1,0:T(8,128)(2,1)S(1)}, bf16[2,32,2048]{2,1,0:T(8,128)(2,1)S(1)}, u32[]{:S(2)}, u32[]{:S(2)}) collective-permute-start(bf16[2,32,2048]{2,1,0:T(8,128)(2,1)S(1)} %collective-permute-done.8.refs_9_), channel_id=1, source_target_pairs={{0,4},{1,17},{4,8},{5,21},{8,12},{9,25},{12,0},{13,29},{16,20},{17... | collective-permute-start | bytes 786440 | tf_op jit(solution)/shard_map/ppermute | solution.py:37
  41.7 10.3 %collective-permute-start.11 = (bf16[1,32,2048]{2,1,0:T(8,128)(2,1)S(1)}, bf16[1,32,2048]{2,1,0:T(8,128)(2,1)S(1)}, u32[]{:S(2)}, u32[]{:S(2)}) collective-permute-start(bf16[1,32,2048]{2,1,0:T(8,128)(2,1)S(1)} %collective-permute-done.6.refs_7_), channel_id=1, source_target_pairs={{0,4},{1,17},{4,8},{5,21},{8,12},{9,25},{12,0},{13,29},{16,20},{17... | collective-permute-start | bytes 393224 | tf_op jit(solution)/shard_map/ppermute | solution.py:37
  44.4 10.2 %collective-permute-start.16 = (bf16[1,32,2048]{2,1,0:T(8,128)(2,1)S(1)}, bf16[1,32,2048]{2,1,0:T(8,128)(2,1)}, u32[]{:S(2)}, u32[]{:S(2)}) collective-permute-start(bf16[1,32,2048]{2,1,0:T(8,128)(2,1)S(1)} %collective-permute-done.6.refs_7_), channel_id=1, source_target_pairs={{0,12},{1,49},{4,0},{5,53},{8,4},{9,57},{12,8},{13,61},{16,28},{17... | collective-permute-start | bytes 393224 | tf_op jit(solution)/shard_map/ppermute | solution.py:37
  48.4 6.2 %collective-permute-start.17 = (bf16[1,32,2048]{2,1,0:T(8,128)(2,1)}, bf16[1,32,2048]{2,1,0:T(8,128)(2,1)}, u32[]{:S(2)}, u32[]{:S(2)}) collective-permute-start(bf16[1,32,2048]{2,1,0:T(8,128)(2,1)} %collective-permute-done.7.refs_8_), channel_id=1, source_target_pairs={{0,12},{1,49},{4,0},{5,53},{8,4},{9,57},{12,8},{13,61},{16,28},{17... | collective-permute-start | bytes 393224 | tf_op jit(solution)/shard_map/ppermute | solution.py:37
  52.0 10.4 %collective-permute-start.19 = (bf16[2,32,2048]{2,1,0:T(8,128)(2,1)}, bf16[2,32,2048]{2,1,0:T(8,128)(2,1)}, u32[]{:S(2)}, u32[]{:S(2)}) collective-permute-start(bf16[2,32,2048]{2,1,0:T(8,128)(2,1)} %collective-permute-done.9.refs_10_), channel_id=1, source_target_pairs={{0,4},{1,17},{4,8},{5,21},{8,12},{9,25},{12,0},{13,29},{16,20},{17... | collective-permute-start | bytes 786440 | tf_op jit(solution)/shard_map/ppermute | solution.py:37
  52.0 10.4 %collective-permute-start.20 = (bf16[2,32,2048]{2,1,0:T(8,128)(2,1)S(1)}, bf16[2,32,2048]{2,1,0:T(8,128)(2,1)}, u32[]{:S(2)}, u32[]{:S(2)}) collective-permute-start(bf16[2,32,2048]{2,1,0:T(8,128)(2,1)S(1)} %collective-permute-done.15.refs_16_), channel_id=1, source_target_pairs={{0,12},{1,49},{4,0},{5,53},{8,4},{9,57},{12,8},{13,61},{16,28},{17... | collective-permute-start | bytes 786440 | tf_op jit(solution)/shard_map/ppermute | solution.py:37
  54.6 6.5 %collective-permute-start.12 = (bf16[1,32,2048]{2,1,0:T(8,128)(2,1)}, bf16[1,32,2048]{2,1,0:T(8,128)(2,1)}, u32[]{:S(2)}, u32[]{:S(2)}) collective-permute-start(bf16[1,32,2048]{2,1,0:T(8,128)(2,1)} %collective-permute-done.7.refs_8_), channel_id=1, source_target_pairs={{0,4},{1,17},{4,8},{5,21},{8,12},{9,25},{12,0},{13,29},{16,20},{17... | collective-permute-start | bytes 393224 | tf_op jit(solution)/shard_map/ppermute | solution.py:37
  54.6 6.5 %collective-permute-start.21 = (bf16[1,32,2048]{2,1,0:T(8,128)(2,1)}, bf16[1,32,2048]{2,1,0:T(8,128)(2,1)}, u32[]{:S(2)}, u32[]{:S(2)}) collective-permute-start(bf16[1,32,2048]{2,1,0:T(8,128)(2,1)} %collective-permute-done.16.refs_17_), channel_id=1, source_target_pairs={{0,12},{1,49},{4,0},{5,53},{8,4},{9,57},{12,8},{13,61},{16,28},{17... | collective-permute-start | bytes 393224 | tf_op jit(solution)/shard_map/ppermute | solution.py:37
  58.0 4.4 %collective-permute-start.22 = (bf16[1,32,2048]{2,1,0:T(8,128)(2,1)}, bf16[1,32,2048]{2,1,0:T(8,128)(2,1)}, u32[]{:S(2)}, u32[]{:S(2)}) collective-permute-start(bf16[1,32,2048]{2,1,0:T(8,128)(2,1)} %collective-permute-done.17.refs_18_), channel_id=1, source_target_pairs={{0,12},{1,49},{4,0},{5,53},{8,4},{9,57},{12,8},{13,61},{16,28},{17... | collective-permute-start | bytes 393224 | tf_op jit(solution)/shard_map/ppermute | solution.py:37
  105.6 20.1 %collective-permute-start.31 = (bf16[144,2048]{1,0:T(8,128)(2,1)}, bf16[144,2048]{1,0:T(8,128)(2,1)S(1)}, u32[]{:S(2)}, u32[]{:S(2)}) collective-permute-start(bf16[144,2048]{1,0:T(8,128)(2,1)} %get-tuple-element.67), channel_id=1, source_target_pairs={{0,4},{1,17},{4,8},{5,21},{8,12},{9,25},{12,0},{13,29},{16,20},{17... | collective-permute-start | bytes 1769480 | tf_op jit(solution)/shard_map/ppermute | solution.py:37
  105.8 15.7 %collective-permute-start.25 = (bf16[128,2048]{1,0:T(8,128)(2,1)}, bf16[128,2048]{1,0:T(8,128)(2,1)}, u32[]{:S(2)}, u32[]{:S(2)}) collective-permute-start(bf16[128,2048]{1,0:T(8,128)(2,1)} %get-tuple-element.58), channel_id=1, source_target_pairs={{0,4},{1,17},{4,8},{5,21},{8,12},{9,25},{12,0},{13,29},{16,20},{17... | collective-permute-start | bytes 1572872 | tf_op jit(solution)/shard_map/ppermute | solution.py:37
  107.2 15.8 %collective-permute-start.26 = (bf16[128,2048]{1,0:T(8,128)(2,1)}, bf16[128,2048]{1,0:T(8,128)(2,1)}, u32[]{:S(2)}, u32[]{:S(2)}) collective-permute-start(bf16[128,2048]{1,0:T(8,128)(2,1)} %get-tuple-element.59), channel_id=1, source_target_pairs={{0,12},{1,49},{4,0},{5,53},{8,4},{9,57},{12,8},{13,61},{16,28},{17... | collective-permute-start | bytes 1572872 | tf_op jit(solution)/shard_map/ppermute | solution.py:37
  108.5 20.8 %collective-permute-start.32 = (bf16[144,2048]{1,0:T(8,128)(2,1)}, bf16[144,2048]{1,0:T(8,128)(2,1)}, u32[]{:S(2)}, u32[]{:S(2)}) collective-permute-start(bf16[144,2048]{1,0:T(8,128)(2,1)} %get-tuple-element.68), channel_id=1, source_target_pairs={{0,12},{1,49},{4,0},{5,53},{8,4},{9,57},{12,8},{13,61},{16,28},{17... | collective-permute-start | bytes 1769480 | tf_op jit(solution)/shard_map/ppermute | solution.py:37
  109.9 42.7 %collective-permute-start.28 = (bf16[128,2048]{1,0:T(8,128)(2,1)}, bf16[128,2048]{1,0:T(8,128)(2,1)}, u32[]{:S(2)}, u32[]{:S(2)}) collective-permute-start(bf16[128,2048]{1,0:T(8,128)(2,1)} %get-tuple-element.61), channel_id=1, source_target_pairs={{0,4},{1,17},{4,8},{5,21},{8,12},{9,25},{12,0},{13,29},{16,20},{17... | collective-permute-start | bytes 1572872 | tf_op jit(solution)/shard_map/ppermute | solution.py:37
  121.5 31.0 %collective-permute-start.29 = (bf16[128,2048]{1,0:T(8,128)(2,1)}, bf16[128,2048]{1,0:T(8,128)(2,1)}, u32[]{:S(2)}, u32[]{:S(2)}) collective-permute-start(bf16[128,2048]{1,0:T(8,128)(2,1)} %get-tuple-element.62), channel_id=1, source_target_pairs={{0,12},{1,49},{4,0},{5,53},{8,4},{9,57},{12,8},{13,61},{16,28},{17... | collective-permute-start | bytes 1572872 | tf_op jit(solution)/shard_map/ppermute | solution.py:37
  125.6 27.0 %collective-permute-start.27 = (bf16[128,2048]{1,0:T(8,128)(2,1)}, bf16[128,2048]{1,0:T(8,128)(2,1)}, u32[]{:S(2)}, u32[]{:S(2)}) collective-permute-start(bf16[128,2048]{1,0:T(8,128)(2,1)} %get-tuple-element.60), channel_id=1, source_target_pairs={{0,4},{1,17},{4,8},{5,21},{8,12},{9,25},{12,0},{13,29},{16,20},{17... | collective-permute-start | bytes 1572872 | tf_op jit(solution)/shard_map/ppermute | solution.py:37
  125.6 30.9 %collective-permute-start.30 = (bf16[128,2048]{1,0:T(8,128)(2,1)}, bf16[128,2048]{1,0:T(8,128)(2,1)}, u32[]{:S(2)}, u32[]{:S(2)}) collective-permute-start(bf16[128,2048]{1,0:T(8,128)(2,1)} %get-tuple-element.63), channel_id=1, source_target_pairs={{0,12},{1,49},{4,0},{5,53},{8,4},{9,57},{12,8},{13,61},{16,28},{17... | collective-permute-start | bytes 1572872 | tf_op jit(solution)/shard_map/ppermute | solution.py:37
  129.3 49.8 %collective-permute-start.23 = (f32[208,1024]{1,0:T(8,128)}, f32[208,1024]{1,0:T(8,128)S(1)}, u32[]{:S(2)}, u32[]{:S(2)}) collective-permute-start(f32[208,1024]{1,0:T(8,128)} %slice_bitcast_fusion), channel_id=1, source_target_pairs={{0,1},{1,0},{4,5},{5,4},{8,9},{9,8},{12,13},{13,12},{16,17},{17,16... | collective-permute-start | bytes 2555912 | tf_op jit(solution)/shard_map/ppermute | solution.py:37
  152.5 17.5 %collective-permute-start.33 = (bf16[144,2048]{1,0:T(8,128)(2,1)}, bf16[144,2048]{1,0:T(8,128)(2,1)}, u32[]{:S(2)}, u32[]{:S(2)}) collective-permute-start(bf16[144,2048]{1,0:T(8,128)(2,1)} %get-tuple-element.69), channel_id=1, source_target_pairs={{0,4},{1,17},{4,8},{5,21},{8,12},{9,25},{12,0},{13,29},{16,20},{17... | collective-permute-start | bytes 1769480 | tf_op jit(solution)/shard_map/ppermute | solution.py:37
  152.5 17.0 %collective-permute-start.34 = (bf16[128,2048]{1,0:T(8,128)(2,1)}, bf16[128,2048]{1,0:T(8,128)(2,1)}, u32[]{:S(2)}, u32[]{:S(2)}) collective-permute-start(bf16[128,2048]{1,0:T(8,128)(2,1)} %get-tuple-element.70), channel_id=1, source_target_pairs={{0,4},{1,17},{4,8},{5,21},{8,12},{9,25},{12,0},{13,29},{16,20},{17... | collective-permute-start | bytes 1572872 | tf_op jit(solution)/shard_map/ppermute | solution.py:37
  152.6 16.9 %collective-permute-start.35 = (bf16[128,2048]{1,0:T(8,128)(2,1)}, bf16[128,2048]{1,0:T(8,128)(2,1)}, u32[]{:S(2)}, u32[]{:S(2)}) collective-permute-start(bf16[128,2048]{1,0:T(8,128)(2,1)} %get-tuple-element.71), channel_id=1, source_target_pairs={{0,12},{1,49},{4,0},{5,53},{8,4},{9,57},{12,8},{13,61},{16,28},{17... | collective-permute-start | bytes 1572872 | tf_op jit(solution)/shard_map/ppermute | solution.py:37
  156.5 13.5 %collective-permute-start.36 = (bf16[128,2048]{1,0:T(8,128)(2,1)}, bf16[128,2048]{1,0:T(8,128)(2,1)}, u32[]{:S(2)}, u32[]{:S(2)}) collective-permute-start(bf16[128,2048]{1,0:T(8,128)(2,1)} %get-tuple-element.72), channel_id=1, source_target_pairs={{0,12},{1,49},{4,0},{5,53},{8,4},{9,57},{12,8},{13,61},{16,28},{17... | collective-permute-start | bytes 1572872 | tf_op jit(solution)/shard_map/ppermute | solution.py:37
  175.1 7.7 %collective-permute-start.37 = (bf16[80,2048]{1,0:T(8,128)(2,1)}, bf16[80,2048]{1,0:T(8,128)(2,1)S(1)}, u32[]{:S(2)}, u32[]{:S(2)}) collective-permute-start(bf16[80,2048]{1,0:T(8,128)(2,1)} %get-tuple-element.78), channel_id=1, source_target_pairs={{0,16},{1,5},{4,20},{5,9},{8,24},{9,13},{12,28},{13,1},{16,32},{17... | collective-permute-start | bytes 983048 | tf_op jit(solution)/shard_map/ppermute | solution.py:37
  175.2 7.6 %collective-permute-start.38 = (bf16[80,2048]{1,0:T(8,128)(2,1)}, bf16[80,2048]{1,0:T(8,128)(2,1)}, u32[]{:S(2)}, u32[]{:S(2)}) collective-permute-start(bf16[80,2048]{1,0:T(8,128)(2,1)} %get-tuple-element.79), channel_id=1, source_target_pairs={{0,48},{1,13},{4,52},{5,1},{8,56},{9,5},{12,60},{13,9},{16,0},{17,... | collective-permute-start | bytes 983048 | tf_op jit(solution)/shard_map/ppermute | solution.py:37
  186.0 11.2 %collective-permute-start.39 = (bf16[144,2048]{1,0:T(8,128)(2,1)}, bf16[144,2048]{1,0:T(8,128)(2,1)S(1)}, u32[]{:S(2)}, u32[]{:S(2)}) collective-permute-start(bf16[144,2048]{1,0:T(8,128)(2,1)} %get-tuple-element.80), channel_id=1, source_target_pairs={{0,16},{1,5},{4,20},{5,9},{8,24},{9,13},{12,28},{13,1},{16,32},{17... | collective-permute-start | bytes 1769480 | tf_op jit(solution)/shard_map/ppermute | solution.py:37
  186.0 11.2 %collective-permute-start.40 = (bf16[128,2048]{1,0:T(8,128)(2,1)}, bf16[128,2048]{1,0:T(8,128)(2,1)S(1)}, u32[]{:S(2)}, u32[]{:S(2)}) collective-permute-start(bf16[128,2048]{1,0:T(8,128)(2,1)} %get-tuple-element.81), channel_id=1, source_target_pairs={{0,48},{1,13},{4,52},{5,1},{8,56},{9,5},{12,60},{13,9},{16,0},{17,... | collective-permute-start | bytes 1572872 | tf_op jit(solution)/shard_map/ppermute | solution.py:37
  190.6 15.0 %collective-permute-start.24 = (f32[144,1024]{1,0:T(8,128)}, f32[144,1024]{1,0:T(8,128)}, u32[]{:S(2)}, u32[]{:S(2)}) collective-permute-start(f32[144,1024]{1,0:T(8,128)} %slice_bitcast_fusion.1), channel_id=1, source_target_pairs={{0,1},{1,0},{4,5},{5,4},{8,9},{9,8},{12,13},{13,12},{16,17},{17,16... | collective-permute-start | bytes 1769480 | tf_op jit(solution)/shard_map/ppermute | solution.py:37
  201.3 9.5 %collective-permute-start.41 = (bf16[80,2560]{1,0:T(8,128)(2,1)}, bf16[80,2560]{1,0:T(8,128)(2,1)S(1)}, u32[]{:S(2)}, u32[]{:S(2)}) collective-permute-start(bf16[80,2560]{1,0:T(8,128)(2,1)} %get-tuple-element.83), channel_id=1, source_target_pairs={{0,64},{1,65},{4,68},{5,69},{8,72},{9,73},{12,76},{13,77},{16,80},... | collective-permute-start | bytes 1228808 | tf_op jit(solution)/shard_map/ppermute | solution.py:37
  201.9 8.9 %collective-permute-start.42 = (bf16[80,2560]{1,0:T(8,128)(2,1)}, bf16[80,2560]{1,0:T(8,128)(2,1)S(1)}, u32[]{:S(2)}, u32[]{:S(2)}) collective-permute-start(bf16[80,2560]{1,0:T(8,128)(2,1)} %get-tuple-element.83), channel_id=1, source_target_pairs={{0,66},{1,67},{4,70},{5,71},{8,74},{9,75},{12,78},{13,79},{16,82},... | collective-permute-start | bytes 1228808 | tf_op jit(solution)/shard_map/ppermute | solution.py:37
  204.0 15.8 %collective-permute-start.43 = (bf16[80,2560]{1,0:T(8,128)(2,1)}, bf16[80,2560]{1,0:T(8,128)(2,1)}, u32[]{:S(2)}, u32[]{:S(2)}) collective-permute-start(bf16[80,2560]{1,0:T(8,128)(2,1)} %get-tuple-element.82.same), channel_id=1, source_target_pairs={{0,2},{1,3},{4,6},{5,7},{8,10},{9,11},{12,14},{13,15},{16,18},{17,... | collective-permute-start | bytes 1228808 | tf_op jit(solution)/shard_map/ppermute | solution.py:37
  222.2 6.5 %collective-permute-start.44 = (f32[72,2560]{1,0:T(8,128)}, f32[72,2560]{1,0:T(8,128)S(1)}, u32[]{:S(2)}, u32[]{:S(2)}) collective-permute-start(f32[72,2560]{1,0:T(8,128)} %shard_map.192.mine), channel_id=1, source_target_pairs={{0,1},{1,0},{4,5},{5,4},{8,9},{9,8},{12,13},{13,12},{16,17},{17,16... | collective-permute-start | bytes 2211848 | tf_op jit(solution)/shard_map/ppermute | solution.py:37
  (40 other events, 438.6 us)
Sparse Core Ops, SparseCore 0:
  10.9 73.8 all-gather.1
where the time goes:
time: 239 us
  starting transfers between devices  85.5 us (36%)
  Pallas kernels  63.8 us (27%)
  waiting for transfers between devices  52.6 us (22%)
  between operations  14.7 us (6%)
  other arithmetic  13 us (5%)
  local copies, waits for them, and re-layouts  9.29 us (4%)
    ppermute x45, starting transfers between devices, send(): return lax.ppermute(value, FSDP_REP, pairs(move))  85.5 us
    ppermute x45, waiting for transfers between devices, send(): return lax.ppermute(value, FSDP_REP, pairs(move))  52.5 us
    pallas_call x2, Pallas kernels, local_compute(): pl.pallas_call(lambda *refs: local_body(length, placed, *refs), in_specs=...  43 us
    pallas_call x7, Pallas kernels, in_one_kernel(): pl.pallas_call(body, in_specs=specs, out_specs=in_vmem(len(shapes)), out_...  20.8 us
  transfers between devices with their start and end apart: 46, of which 18 were waited for; matrix products, arithmetic and copies ran while one was open for 7% of the time, Pallas kernels for 15%

commit v1 on v0

--- a/solution.py
+++ b/solution.py
@@ -95,7 +95,7 @@
     n_weights = 2 if placed else 20
     weights, refs = refs[:n_weights], refs[n_weights:]
     grads, refs = refs[:7], refs[7:]
-    dh, gain_part, refs = refs[0], refs[1], refs[2:]
+    dh, gain_part, refs = refs[:2], refs[2], refs[3:]
     if placed:
         before, weights = weights[1], weights[:1]
     hidden, hidden_t, dyb, qkv, datt, att, dqkv, gqkv, gout, wqkv, wout = refs
@@ -130,19 +130,17 @@
         dyb[b * size : (b + 1) * size, :] = pair[1]
     hidden_t[...] = hidden[...].T
 
-    @pl.loop(0, 6)
-    def _(n):
-        at = pl.multiple_of(n * 256, 256)
-        qkv[:, pl.ds(at, 256)] = dot_nn(hidden[...], w_qkv(n)).astype(bf16)
+    for n in range(6):
+        qkv[:, 256 * n : 256 * n + 256] = dot_nn(hidden[...], w_qkv(n)).astype(bf16)
 
     datt[...] = (dot_nt(dyb[:, :512], w_out(0)) + dot_nt(dyb[:, 512:], w_out(1))).astype(bf16)
 
-    scale = HEAD ** (-0.5)
+    scale = jnp.asarray(HEAD ** (-0.5), bf16)
     lane = lax.broadcasted_iota(jnp.int32, (size, 128), 1)
     key_at = lax.broadcasted_iota(jnp.int32, (size, size), 1)
     zero = jnp.zeros((), bf16)
 
-    @pl.loop(0, 8)
+    @pl.loop(0, 8, unroll=2)
     def _(n):
         r = pl.ds(pl.multiple_of((n // 4) * size, 16), size)
         at = pl.multiple_of((n % 4) * 128, 128)
@@ -153,11 +151,11 @@
         sums = [None] * 4
         for head in range(2):
             mine = (lane < HEAD) if head == 0 else (lane >= HEAD)
-            q = jnp.where(mine, query, zero)
-            k = jnp.where(mine, keyed, zero)
+            q = jnp.where(mine, query * scale, zero)
+            k = jnp.where(mine, keyed * scale, zero)
             v = jnp.where(mine, valued, zero)
             d = jnp.where(mine, dout, zero)
-            score = dot_nt(q, keyed) * scale
+            score = dot_nt(q, keyed)
             score = jnp.where(key_at < length, score, -1e30)
             top = jnp.max(score, axis=1, keepdims=True)
             grown = jnp.exp(score - top)
@@ -165,7 +163,7 @@
             pb = probs.astype(bf16)
             dprob = dot_nt(d, valued)
             inner = jnp.sum(probs * dprob, axis=1, keepdims=True)
-            dsb = (probs * (dprob - inner) * scale).astype(bf16)
+            dsb = (probs * (dprob - inner)).astype(bf16)
             parts = (dot_nn(pb, v), dot_nn(dsb, k), dot_tn(dsb, q), dot_tn(pb, d))
             sums = [p if t is None else t + p for t, p in zip(sums, parts)]
         att[r, pl.ds(at, 128)] = sums[0].astype(bf16)
@@ -179,10 +177,7 @@
             att_t, dyb[:, 512 * half : 512 * half + 512]
         ).astype(bf16)
 
-    @pl.loop(0, 6)
-    def _(n):
-        at = pl.multiple_of(n * 256, 256)
-        gqkv[:, pl.ds(at, 256)] = dot_nn(hidden_t[...], dqkv[:, pl.ds(at, 256)]).astype(bf16)
+    gqkv[...] = dot_nn(hidden_t[...], dqkv[...]).astype(bf16)
 
     for n, ref in enumerate(grads):
         for k, block in enumerate(GRAD_BLOCKS[n]):
@@ -195,7 +190,7 @@
         total = dot_nt(dqkv[b * size : (b + 1) * size, :256], w_qkv(0))
         for k in range(1, 6):
             total = total + dot_nt(dqkv[b * size : (b + 1) * size, k * 256 : k * 256 + 256], w_qkv(k))
-        dh[b] = total
+        dh[b][...] = total
         z = pair[0].astype(f32)
         normed = z * lax.rsqrt(jnp.mean(z * z, axis=1, keepdims=True) + 1e-06)
         part = part + jnp.sum(total * normed, axis=0, keepdims=True)
@@ -237,12 +232,13 @@
     return pl.pallas_call(
         lambda *refs: local_body(length, placed, *refs),
         in_specs=[in_smem()] + in_vmem(3 + len(weights)),
-        out_specs=in_vmem(9),
+        out_specs=in_vmem(10),
         out_shape=[jax.ShapeDtypeStruct((256, 2048), bf16)]
         + [jax.ShapeDtypeStruct((128, 2048), bf16)] * 4
         + [jax.ShapeDtypeStruct((144 if placed else 128, 2048), bf16)] * 2
         + [
-            jax.ShapeDtypeStruct((2, size, 1024), f32),
+            jax.ShapeDtypeStruct((size, 1024), f32),
+            jax.ShapeDtypeStruct((size, 1024), f32),
             jax.ShapeDtypeStruct((1, 2048 if placed else 1024), f32),
         ],
         scratch_shapes=[
@@ -353,26 +349,27 @@
     return (own + far) + (left + right)
 
 
-def fold_last(v_own, v_up_a, v_up_b, v_down_a, v_down_b, own, up_a, up_b, down_a, down_b,
-              gain, up_far, down_far, far_up, far_down, right, left, home, gain_out):
-    parts = (
-        (v_own, v_up_a, v_up_b, v_down_a, v_down_b),
-        (own, up_a, up_b, down_a, down_b),
-    )
-    for s, (o, ua, ub, da, db) in enumerate(parts):
+def fold_sum(own, up_a, up_b, down_a, down_b, out):
+    out[:128, :] = add(own[:128, :], up_a[:128, :], down_a[:128, :]).astype(bf16)
+    out[128:, :] = add(own[128:, :], up_b[...], down_b[...]).astype(bf16)
+
+
+def fold_last(video, own, up_a, up_b, down_a, down_b, gain, up_far, down_far,
+              far_up, far_down, right, left, home, gain_out):
+    for s in range(2):
         for j in range(8):
-            u, d, at = (ua, da, 32 * j) if j < 4 else (ub, db, 32 * j - 128)
-            total = add(o[32 * j : 32 * j + 32, :], u[at : at + 32, :], d[at : at + 32, :])
+            u, d, at = (up_a, down_a, 32 * j) if j < 4 else (up_b, down_b, 32 * j - 128)
+            if s == 0:
+                total = video[32 * j : 32 * j + 32, :].astype(f32)
+            else:
+                total = add(own[32 * j : 32 * j + 32, :], u[at : at + 32, :], d[at : at + 32, :])
             if j < 2:
                 home[64 * s + 32 * j : 64 * s + 32 * j + 32, :] = total
+            elif j < 6:
+                row = 64 * s + 32 * (j % 2)
+                (left if j < 4 else right)[row : row + 32, :] = total.astype(bf16)
             else:
-                ref = (left, right, None)[(j - 2) // 2]
-                if ref is None:
-                    ref = far_up if j == 6 else far_down
-                    ref[32 * s : 32 * s + 32, :] = total.astype(bf16)
-                else:
-                    row = 64 * s + 32 * (j % 2)
-                    ref[row : row + 32, :] = total.astype(bf16)
+                (far_up if j == 6 else far_down)[32 * s : 32 * s + 32, :] = total.astype(bf16)
     total = ring_sum(
         gain[...],
         from_pieces(up_far[128:144, :]),
@@ -417,8 +414,8 @@
     )
     gain_out[...] = total
     for ref in (same, cross):
-        ref[64:80, :2048] = in_pieces(total)
-        ref[64:80, 2048:] = jnp.zeros((16, 512), bf16)
+        ref[64:72, :2048] = in_pieces(total)[:8]
+        ref[64:72, 2048:] = jnp.zeros((8, 512), bf16)
 
 
 def fold_y(count, same, up, down, far, gain, out):
@@ -426,9 +423,9 @@
     out[:64, :] = total / count
     total = ring_sum(
         gain[...],
-        from_pieces(up[64:80, :2048]),
-        from_pieces(down[64:80, :2048]),
-        from_pieces(far[64:80, :2048]),
+        from_pieces(up[64:72, :2048]),
+        from_pieces(down[64:72, :2048]),
+        from_pieces(far[64:72, :2048]),
     )
     out[64:72, :2048] = jnp.broadcast_to(total, (8, 2048))
     out[64:72, 2048:] = jnp.zeros((8, 512), f32)
@@ -452,12 +449,13 @@
 
 def last_steps(video, audio, audio_parts, gain, where, count):
     audio_far = audio_parts[3:5]
+    (video_sum,) = in_one_kernel(fold_sum, [((256, 2048), bf16)], *video)
     far_up, far_down, right, left, home, gain = in_one_kernel(
         fold_last,
         [((80, 2048), bf16)] * 2
         + [((128, 2048), bf16)] * 2
         + [((128, 2048), f32), ((1, 2048), f32)],
-        *video,
+        video_sum,
         *audio,
         gain,
         *audio_far,
@@ -471,7 +469,7 @@
     down = send(left, along_mid(-1))
     same, cross, gain = in_one_kernel(
         fold_mid,
-        [((80, 2560), bf16)] * 2 + [((1, 2048), f32)],
+        [((72, 2560), bf16)] * 2 + [((1, 2048), f32)],
         home,
         gain,
         up,
@@ -505,15 +503,16 @@
     return own, send(own, to_partner)
 
 
-def finish(own, gain, dh):
-    dhidden = dh[0] + send(dh[1], to_partner)
+def finish(own, gain, dh, dh_peer):
+    from_peer = send(dh_peer, to_partner)
+    dhidden = dh + from_peer
     z = own[0].astype(f32)
     inverse = lax.rsqrt(jnp.mean(z * z, axis=1, keepdims=True) + 1e-06)
     normed = z * inverse
     dnorm = dhidden * gain
     d_out = own[1].astype(f32)
-    d_z = d_out + inverse * (dnorm - normed * jnp.mean(dnorm * normed, axis=1, keepdims=True))
-    return d_z
+    mean = jnp.mean(dnorm * normed, axis=1, keepdims=True)
+    return d_out + inverse * (dnorm - normed * mean)
 
 
 def per_device(
@@ -540,11 +539,11 @@
     vown, vpeer = clip_pair(video_in[0], bottle_in[0], grad_video[0], grad_bottle[0])
     aown, apeer = clip_pair(audio_in[0], bottle_in[0], grad_audio[0], grad_bottle[0])
     vpeer, apeer = lax.optimization_barrier((vpeer, apeer))
-    *grads, dh_video, gain_v = local_compute(
+    *grads, dh_video, dh_video_peer, gain_v = local_compute(
         video_len + bottle_len, False, where, vown, vpeer, video_gain, vweights
     )
     video_parts = first_steps(grads)
-    *grads, dh_audio, gain = local_compute(
+    *grads, dh_audio, dh_audio_peer, gain = local_compute(
         audio_len + bottle_len,
         True,
         where,
@@ -564,8 +563,8 @@
         gain_v,
         gain_a,
     ) = last_steps(video, audio, audio_parts, gain, where, count)
-    dz_video = finish(vown, video_gain, dh_video)
-    dz_audio = finish(aown, audio_gain, dh_audio)
+    dz_video = finish(vown, video_gain, dh_video, dh_video_peer)
+    dz_audio = finish(aown, audio_gain, dh_audio, dh_audio_peer)
     video_end = video_len + bottle_len
     audio_end = audio_len + bottle_len
     dvideo_in = dz_video[None, :video_len].astype(bf16)

time: 239 us -> 235 us (0.983)
  Pallas kernels: 63.8 us -> 57 us
    pallas_call x2, Pallas kernels: 43 us -> 34.1 us  [local_compute(): pl.pallas_call(lambda *refs: local_body(length, placed, *refs), in_specs=...]
    squeeze x2 -> x0, local copies, waits for them, and re-layouts: 2.88 us -> none  [finish(): dhidden = dh[0] + send(dh[1], to_partner)]
    pallas_call x7 -> x8, Pallas kernels: 20.8 us -> 22.9 us  [in_one_kernel(): pl.pallas_call(body, in_specs=specs, out_specs=in_vmem(len(shapes)), out_...]
  transfers between devices with their start and end apart: 46 -> 46, of which waited for: 18 -> 18; matrix products, arithmetic and copies ran while one was open for 7% -> 6% of each run, Pallas kernels for 15% -> 15%
where the time goes in v1:
time: 235 us; the launch traced here: 234 us
  starting transfers between devices  86.3 us (37%)
  Pallas kernels  57 us (24%)
  waiting for transfers between devices  53.9 us (23%)
  between operations  14.6 us (6%)
  other arithmetic  12.4 us (5%)
  local copies, waits for them, and re-layouts  9.74 us (4%)
    ppermute x45, starting transfers between devices, send(): return lax.ppermute(value, FSDP_REP, pairs(move))  86.2 us
    ppermute x45, waiting for transfers between devices, send(): return lax.ppermute(value, FSDP_REP, pairs(move))  52.4 us
    pallas_call x2, Pallas kernels, local_compute(): pl.pallas_call(lambda *refs: local_body(length, placed, *refs), in_specs=...  34.1 us
    pallas_call x8, Pallas kernels, in_one_kernel(): pl.pallas_call(body, in_specs=specs, out_specs=in_vmem(len(shapes)), out_...  22.9 us
  transfers between devices with their start and end apart: 46, of which 18 were waited for; matrix products, arithmetic and copies ran while one was open for 6% of the time, Pallas kernels for 15%

profile of v1, /device:TPU:1, one launch (start us, length us, event | category | flops | bytes accessed | tf_op | source)
XLA Modules:
  0.0 234.0 jit_solution(10181989179159288922)
XLA Ops:
  8.9 1.5 fusion.18
  12.8 2.2 collective-permute-start.2
  19.4 2.5 %collective-permute-done.3 = bf16[16,2560]{1,0:T(8,128)(2,1)S(1)} collective-permute-done((bf16[16,2560]{1,0:T(8,128)(2,1)S(1)}, bf16[16,2560]{1,0:T(8,128)(2,1)S(1)}, u32[]{:S(2)}, u32[]{:S(2)}) %collective-permute-start.3) | collective-permute-done | bytes 81952 | tf_op jit(solution)/shard_map/ppermute | solution.py:37
  23.7 1.5 collective-permute-start.5
  25.2 1.6 collective-permute-start.8
  26.9 2.3 collective-permute-start
  29.2 3.8 %collective-permute-start.13 = (bf16[2,32,2048]{2,1,0:T(8,128)(2,1)S(1)}, bf16[2,32,2048]{2,1,0:T(8,128)(2,1)S(1)}, u32[]{:S(2)}, u32[]{:S(2)}) collective-permute-start(bf16[2,32,2048]{2,1,0:T(8,128)(2,1)S(1)} %pad_maximum_fusion.2.refs_4_), channel_id=1, source_target_pairs={{0,12},{1,49},{4,0},{5,53},{8,4},{9,57},{12,8},{13,61},{16,28},{17... | collective-permute-start | bytes 786440 | tf_op jit(solution)/shard_map/ppermute | solution.py:37
  33.1 1.5 collective-permute-done.8.refs_9_
  37.9 1.9 collective-permute-done.6.refs_7_
  39.8 1.4 collective-permute-done.7.refs_8_
  41.2 2.9 %collective-permute-start.14 = (bf16[2,32,2048]{2,1,0:T(8,128)(2,1)S(1)}, bf16[2,32,2048]{2,1,0:T(8,128)(2,1)S(1)}, u32[]{:S(2)}, u32[]{:S(2)}) collective-permute-start(bf16[2,32,2048]{2,1,0:T(8,128)(2,1)S(1)} %collective-permute-done.4.refs_5_), channel_id=1, source_target_pairs={{0,12},{1,49},{4,0},{5,53},{8,4},{9,57},{12,8},{13,61},{16,28},{17... | collective-permute-start | bytes 786440 | tf_op jit(solution)/shard_map/ppermute | solution.py:37
  44.1 1.4 collective-permute-start.18
  46.2 3.9 %collective-permute-done.14.refs_15_ = bf16[2,32,2048]{2,1,0:T(8,128)(2,1)S(1)} collective-permute-done((bf16[2,32,2048]{2,1,0:T(8,128)(2,1)S(1)}, bf16[2,32,2048]{2,1,0:T(8,128)(2,1)S(1)}, u32[]{:S(2)}, u32[]{:S(2)}) %collective-permute-start.14) | collective-permute-done | bytes 262176 | tf_op jit(solution)/shard_map/ppermute | solution.py:37
  50.1 3.5 %collective-permute-start.16 = (bf16[1,32,2048]{2,1,0:T(8,128)(2,1)S(1)}, bf16[1,32,2048]{2,1,0:T(8,128)(2,1)}, u32[]{:S(2)}, u32[]{:S(2)}) collective-permute-start(bf16[1,32,2048]{2,1,0:T(8,128)(2,1)S(1)} %collective-permute-done.6.refs_7_), channel_id=1, source_target_pairs={{0,12},{1,49},{4,0},{5,53},{8,4},{9,57},{12,8},{13,61},{16,28},{17... | collective-permute-start | bytes 393224 | tf_op jit(solution)/shard_map/ppermute | solution.py:37
  54.3 3.5 %collective-permute-start.17 = (bf16[1,32,2048]{2,1,0:T(8,128)(2,1)}, bf16[1,32,2048]{2,1,0:T(8,128)(2,1)}, u32[]{:S(2)}, u32[]{:S(2)}) collective-permute-start(bf16[1,32,2048]{2,1,0:T(8,128)(2,1)} %collective-permute-done.7.refs_8_), channel_id=1, source_target_pairs={{0,12},{1,49},{4,0},{5,53},{8,4},{9,57},{12,8},{13,61},{16,28},{17... | collective-permute-start | bytes 393224 | tf_op jit(solution)/shard_map/ppermute | solution.py:37
  57.9 2.7 %collective-permute-start.20 = (bf16[2,32,2048]{2,1,0:T(8,128)(2,1)}, bf16[2,32,2048]{2,1,0:T(8,128)(2,1)}, u32[]{:S(2)}, u32[]{:S(2)}) collective-permute-start(bf16[2,32,2048]{2,1,0:T(8,128)(2,1)} %collective-permute-done.15.refs_16_), channel_id=1, source_target_pairs={{0,12},{1,49},{4,0},{5,53},{8,4},{9,57},{12,8},{13,61},{16,28},{17... | collective-permute-start | bytes 786440 | tf_op jit(solution)/shard_map/ppermute | solution.py:37
  60.5 2.8 %collective-permute-start.21 = (bf16[1,32,2048]{2,1,0:T(8,128)(2,1)}, bf16[1,32,2048]{2,1,0:T(8,128)(2,1)}, u32[]{:S(2)}, u32[]{:S(2)}) collective-permute-start(bf16[1,32,2048]{2,1,0:T(8,128)(2,1)} %collective-permute-done.16.refs_17_), channel_id=1, source_target_pairs={{0,12},{1,49},{4,0},{5,53},{8,4},{9,57},{12,8},{13,61},{16,28},{17... | collective-permute-start | bytes 393224 | tf_op jit(solution)/shard_map/ppermute | solution.py:37
  64.3 1.7 collective-permute-done.12.refs_13_
  66.0 3.1 %collective-permute-done.22.refs_23_ = bf16[1,32,2048]{2,1,0:T(8,128)(2,1)} collective-permute-done((bf16[1,32,2048]{2,1,0:T(8,128)(2,1)}, bf16[1,32,2048]{2,1,0:T(8,128)(2,1)}, u32[]{:S(2)}, u32[]{:S(2)}) %collective-permute-start.22) | collective-permute-done | bytes 131104 | tf_op jit(solution)/shard_map/ppermute | solution.py:37
  69.1 17.4 %local_pieces.1 = (bf16[256,2048]{1,0:T(8,128)(2,1)}, bf16[128,2048]{1,0:T(8,128)(2,1)}, bf16[128,2048]{1,0:T(8,128)(2,1)}, bf16[128,2048]{1,0:T(8,128)(2,1)}, b...) custom-call(s32[4]{0:T(128)} %pad_add_fusion.refs_0_.where, ...), custom_call_target="tpu_custom_call" | custom-call | tf_op jit(solution)/shard_map/local_pieces/pallas_call | solution.py:232
  86.5 1.5 all-gather.2.cloned.1.call-done.refs_4_
  88.0 16.7 %local_placed.1 = (bf16[256,2048]{1,0:T(8,128)(2,1)}, bf16[128,2048]{1,0:T(8,128)(2,1)}, bf16[128,2048]{1,0:T(8,128)(2,1)}, bf16[128,2048]{1,0:T(8,128)(2,1)}, b...) custom-call(s32[4]{0:T(128)} %pad_add_fusion.refs_0_.where, ...), custom_call_target="tpu_custom_call" | custom-call | tf_op jit(solution)/shard_map/local_placed/pallas_call | solution.py:232
  105.4 1.5 collective-permute-start.25
  109.5 11.1 %collective-permute-done.25.up = bf16[128,2048]{1,0:T(8,128)(2,1)S(1)} collective-permute-done((bf16[128,2048]{1,0:T(8,128)(2,1)}, bf16[128,2048]{1,0:T(8,128)(2,1)S(1)}, u32[]{:S(2)}, u32[]{:S(2)}) %collective-permute-start.25) | collective-permute-done | bytes 524320 | tf_op jit(solution)/shard_map/ppermute | solution.py:37
  120.6 1.5 collective-permute-start.29
  122.9 2.7 %shard_map.187 = (bf16[128,2048]{1,0:T(8,128)(2,1)}, bf16[128,2048]{1,0:T(8,128)(2,1)}) custom-call(bf16[128,2048]{1,0:T(8,128)(2,1)} %get-tuple-element.60.right, bf16[128,2048]{1,0:T(8,128)(2,1)} %get-tuple-element.61.left, bf16[128,2048]{1,0:T(8,128)(2,1)} %copy-done.17, bf16[128,2048]{1,0:T(8,128)(2,1)} %copy-done.18), custom_call_target="tpu_custom_call" | custom-call | tf_op jit(solution)/shard_map/pallas_call | solution.py:314
  125.6 2.7 %collective-permute-start.30 = (bf16[128,2048]{1,0:T(8,128)(2,1)}, bf16[128,2048]{1,0:T(8,128)(2,1)}, u32[]{:S(2)}, u32[]{:S(2)}) collective-permute-start(bf16[128,2048]{1,0:T(8,128)(2,1)} %get-tuple-element.67), channel_id=1, source_target_pairs={{0,12},{1,49},{4,0},{5,53},{8,4},{9,57},{12,8},{13,61},{16,28},{17... | collective-permute-start | bytes 1572872 | tf_op jit(solution)/shard_map/ppermute | solution.py:37
  128.2 18.9 %collective-permute-start.23 = (f32[208,1024]{1,0:T(8,128)}, f32[208,1024]{1,0:T(8,128)S(1)}, u32[]{:S(2)}, u32[]{:S(2)}) collective-permute-start(f32[208,1024]{1,0:T(8,128)} %get-tuple-element.54), channel_id=1, source_target_pairs={{0,1},{1,0},{4,5},{5,4},{8,9},{9,8},{12,13},{13,12},{16,17},{17,16... | collective-permute-start | bytes 2555912 | tf_op jit(solution)/shard_map/ppermute | solution.py:37
  147.2 2.7 %shard_map.189 = (bf16[144,2048]{1,0:T(8,128)(2,1)}, bf16[128,2048]{1,0:T(8,128)(2,1)}) custom-call(bf16[128,2048]{1,0:T(8,128)(2,1)} %get-tuple-element.69.right, bf16[128,2048]{1,0:T(8,128)(2,1)} %get-tuple-element.70.left, bf16[144,2048]{1,0:T(8,128)(2,1)} %copy-done.6, bf16[144,2048]{1,0:T(8,128)(2,1)} %copy-done.7), custom_call_target="tpu_custom_call" | custom-call | tf_op jit(solution)/shard_map/pallas_call | solution.py:314
  151.3 1.4 collective-permute-start.35
  152.7 1.4 collective-permute-start.36
  154.6 3.2 %shard_map.188.video = bf16[256,2048]{1,0:T(8,128)(2,1)} custom-call(bf16[256,2048]{1,0:T(8,128)(2,1)} %get-tuple-element.59.own, bf16[128,2048]{1,0:T(8,128)(2,1)} %copy-done.19, bf16[128,2048]{1,0:T(8,128)(2,1)} %collective-permute-done.28.up_b, bf16[128,2048]{1,0:T(8,128)(2,1)} %collective-permute-done.29.down_a, ...), custom_call_target="tpu_custom_call" | custom-call | tf_op jit(solution)/shard_map/pallas_call | solution.py:314
  157.8 8.3 %collective-permute-done.34.up_b = bf16[128,2048]{1,0:T(8,128)(2,1)} collective-permute-done((bf16[128,2048]{1,0:T(8,128)(2,1)}, bf16[128,2048]{1,0:T(8,128)(2,1)}, u32[]{:S(2)}, u32[]{:S(2)}) %collective-permute-start.34) | collective-permute-done | bytes 524320 | tf_op jit(solution)/shard_map/ppermute | solution.py:37
  167.0 4.2 %shard_map.190 = (bf16[80,2048]{1,0:T(8,128)(2,1)}, bf16[80,2048]{1,0:T(8,128)(2,1)}, bf16[128,2048]{1,0:T(8,128)(2,1)}, bf16[128,2048]{1,0:T(8,128)(2,1)}, f32[128,2048]{1,0:T(8,128)}, /*index=5*/f32[1,2048]{1,0:T(1,128)}) custom-call(bf16[256,2048]{1,0:T(8,128)(2,1)} %shard_map.188.video, bf16[256,2048]{1,0:T(8,128)(2,1)} %get-tuple-element.68.own, ...), custom_call_target="tpu_custom_call" | custom-call | tf_op jit(solution)/shard_map/pallas_call | solution.py:314
  171.2 2.7 %collective-permute-start.38 = (bf16[80,2048]{1,0:T(8,128)(2,1)}, bf16[80,2048]{1,0:T(8,128)(2,1)}, u32[]{:S(2)}, u32[]{:S(2)}) collective-permute-start(bf16[80,2048]{1,0:T(8,128)(2,1)} %get-tuple-element.83), channel_id=1, source_target_pairs={{0,48},{1,13},{4,52},{5,1},{8,56},{9,5},{12,60},{13,9},{16,0},{17,... | collective-permute-start | bytes 983048 | tf_op jit(solution)/shard_map/ppermute | solution.py:37
  175.4 4.1 %collective-permute-start.24 = (f32[144,1024]{1,0:T(8,128)}, f32[144,1024]{1,0:T(8,128)S(1)}, u32[]{:S(2)}, u32[]{:S(2)}) collective-permute-start(f32[144,1024]{1,0:T(8,128)} %get-tuple-element.58), channel_id=1, source_target_pairs={{0,1},{1,0},{4,5},{5,4},{8,9},{9,8},{12,13},{13,12},{16,17},{17,16... | collective-permute-start | bytes 1769480 | tf_op jit(solution)/shard_map/ppermute | solution.py:37
  179.4 2.5 %shard_map.191 = (bf16[144,2048]{1,0:T(8,128)(2,1)}, bf16[128,2048]{1,0:T(8,128)(2,1)}) custom-call(bf16[128,2048]{1,0:T(8,128)(2,1)} %get-tuple-element.80.right, bf16[128,2048]{1,0:T(8,128)(2,1)} %get-tuple-element.81.left, bf16[80,2048]{1,0:T(8,128)(2,1)} %collective-permute-done.37.up.up_far, bf16[80,2048]{1,0:T(8,128)(2,1)} %collective-permute-done.38.down.down_far), custom_call_target="tpu_custom_call" | custom-call | tf_op jit(solution)/shard_map/pallas_call | solution.py:314
  182.6 2.7 %collective-permute-start.40 = (bf16[128,2048]{1,0:T(8,128)(2,1)}, bf16[128,2048]{1,0:T(8,128)(2,1)}, u32[]{:S(2)}, u32[]{:S(2)}) collective-permute-start(bf16[128,2048]{1,0:T(8,128)(2,1)} %get-tuple-element.85), channel_id=1, source_target_pairs={{0,48},{1,13},{4,52},{5,1},{8,56},{9,5},{12,60},{13,9},{16,0},{17,... | collective-permute-start | bytes 1572872 | tf_op jit(solution)/shard_map/ppermute | solution.py:37
  185.3 1.4 fusion.5
  188.4 3.3 %collective-permute-done.40.down = bf16[128,2048]{1,0:T(8,128)(2,1)} collective-permute-done((bf16[128,2048]{1,0:T(8,128)(2,1)}, bf16[128,2048]{1,0:T(8,128)(2,1)}, u32[]{:S(2)}, u32[]{:S(2)}) %collective-permute-start.40) | collective-permute-done | bytes 524320 | tf_op jit(solution)/shard_map/ppermute | solution.py:37
  192.5 2.9 %shard_map.192 = (bf16[72,2560]{1,0:T(8,128)(2,1)}, bf16[72,2560]{1,0:T(8,128)(2,1)}, f32[1,2048]{1,0:T(1,128)}) custom-call(s32[4]{0:T(128)} %pad_add_fusion.refs_0_.where, f32[128,2048]{1,0:T(8,128)} %get-tuple-element.78.home, f32[1,2048]{1,0:T(1,128)} %get-tuple-element.79.gain, bf16[144,2048]{1,0:T(8,128)(2,1)} %collective-permute-done.39.up, ...), custom_call_target="tpu_custom_call" | custom-call | tf_op jit(solution)/shard_map/pallas_call | solution.py:314
  195.4 1.8 collective-permute-start.41
  200.7 2.9 %collective-permute-done.41.up = bf16[72,2560]{1,0:T(8,128)(2,1)S(1)} collective-permute-done((bf16[72,2560]{1,0:T(8,128)(2,1)}, bf16[72,2560]{1,0:T(8,128)(2,1)S(1)}, u32[]{:S(2)}, u32[]{:S(2)}) %collective-permute-start.41) | collective-permute-done | bytes 368672 | tf_op jit(solution)/shard_map/ppermute | solution.py:37
  203.7 7.7 %collective-permute-done.43.far = bf16[72,2560]{1,0:T(8,128)(2,1)S(1)} collective-permute-done((bf16[72,2560]{1,0:T(8,128)(2,1)}, bf16[72,2560]{1,0:T(8,128)(2,1)S(1)}, u32[]{:S(2)}, u32[]{:S(2)}) %collective-permute-start.43) | collective-permute-done | bytes 368672 | tf_op jit(solution)/shard_map/ppermute | solution.py:37
  212.2 2.4 %shard_map.193.mine = f32[72,2560]{1,0:T(8,128)} custom-call(bf16[72,2560]{1,0:T(8,128)(2,1)} %get-tuple-element.86.same, bf16[72,2560]{1,0:T(8,128)(2,1)} %copy-done.21, bf16[72,2560]{1,0:T(8,128)(2,1)} %copy-done.22, bf16[72,2560]{1,0:T(8,128)(2,1)} %copy-done.23, f32[1,2048]{1,0:T(1,128)} %get-tuple-element.88.gain), custom_call_target="tpu_custom_call" | custom-call | tf_op jit(solution)/shard_map/pallas_call | solution.py:314
  214.6 5.8 %collective-permute-start.44 = (f32[72,2560]{1,0:T(8,128)}, f32[72,2560]{1,0:T(8,128)S(1)}, u32[]{:S(2)}, u32[]{:S(2)}) collective-permute-start(f32[72,2560]{1,0:T(8,128)} %shard_map.193.mine), channel_id=1, source_target_pairs={{0,1},{1,0},{4,5},{5,4},{8,9},{9,8},{12,13},{13,12},{16,17},{17,16... | collective-permute-start | bytes 2211848 | tf_op jit(solution)/shard_map/ppermute | solution.py:37
  221.7 1.5 fusion.21
  224.8 2.4 %shard_map.194 = (f32[32,3072]{1,0:T(8,128)}, f32[32,1024]{1,0:T(8,128)}, f32[32,3072]{1,0:T(8,128)}, f32[32,1024]{1,0:T(8,128)}, f32[1,1024]{1,0:T(1,128)}, /*index=5*/f32[1,1024]{1,0:T(1,128)}) custom-call(s32[4]{0:T(128)} %pad_add_fusion.refs_0_.where, f32[72,2560]{1,0:T(8,128)} %shard_map.193.mine, f32[72,2560]{1,0:T(8,128)} %copy-done.13), custom_call_target="tpu_custom_call" | custom-call | tf_op jit(solution)/shard_map/pallas_call | solution.py:314
  (171 shorter events, 34.5 us)
Async XLA Ops:
  7.2 80.8 %all-gather.2.cloned.1.call-start = ((), (), s32[]{:S(2)}) async-start(), calls=%async_computation | async-start | bytes 5324800 | tf_op jit(solution)/shard_map/all_gather | solution.py:271
  12.8 6.7 %collective-permute-start.2 = (bf16[16,2560]{1,0:T(8,128)(2,1)S(1)}, bf16[16,2560]{1,0:T(8,128)(2,1)S(1)}, u32[]{:S(2)}, u32[]{:S(2)}) collective-permute-start(bf16[16,2560]{1,0:T(8,128)(2,1)S(1)} %get-tuple-element.102), channel_id=1, source_target_pairs={{0,64},{1,65},{4,68},{5,69},{8,72},{9,73},{12,76},{13,77},{16,80},... | collective-permute-start | bytes 245768 | tf_op jit(solution)/shard_map/ppermute | solution.py:37
  15.0 139.1 %copy-start.34 = (bf16[144]{0:T(256)(128)(2,1)}, bf16[144]{0:T(256)(128)(2,1)S(1)}, u32[]{:S(2)}) copy-start(bf16[144]{0:T(256)(128)(2,1)S(1)} %pad.15.clone) | copy-start | bytes 868
  17.0 27.0 %collective-permute-start.1 = (bf16[2,144,1024]{2,1,0:T(8,128)(2,1)S(1)}, bf16[2,144,1024]{2,1,0:T(8,128)(2,1)}, u32[]{:S(2)}, u32[]{:S(2)}) collective-permute-start(bf16[2,144,1024]{2,1,0:T(8,128)(2,1)S(1)} %pad_maximum_fusion.1.refs_1_), channel_id=1, source_target_pairs={{0,1},{1,0},{4,5},{5,4},{8,9},{9,8},{12,13},{13,12},{16,17},{17,16... | collective-permute-start | bytes 1769480 | tf_op jit(solution)/shard_map/ppermute | solution.py:37
  18.1 3.9 %collective-permute-start.3 = (bf16[16,2560]{1,0:T(8,128)(2,1)S(1)}, bf16[16,2560]{1,0:T(8,128)(2,1)S(1)}, u32[]{:S(2)}, u32[]{:S(2)}) collective-permute-start(bf16[16,2560]{1,0:T(8,128)(2,1)S(1)} %get-tuple-element.101), channel_id=1, source_target_pairs={{0,66},{1,67},{4,70},{5,71},{8,74},{9,75},{12,78},{13,79},{16,82},... | collective-permute-start | bytes 245768 | tf_op jit(solution)/shard_map/ppermute | solution.py:37
  19.4 155.0 %copy-start.35 = (bf16[208]{0:T(256)(128)(2,1)}, bf16[208]{0:T(256)(128)(2,1)S(1)}, u32[]{:S(2)}) copy-start(bf16[208]{0:T(256)(128)(2,1)S(1)} %pad.27.clone) | copy-start | bytes 1252
  22.1 7.1 %collective-permute-start.4 = (bf16[2,32,2048]{2,1,0:T(8,128)(2,1)S(1)}, bf16[2,32,2048]{2,1,0:T(8,128)(2,1)S(1)}, u32[]{:S(2)}, u32[]{:S(2)}) collective-permute-start(bf16[2,32,2048]{2,1,0:T(8,128)(2,1)S(1)} %pad_maximum_fusion.2.refs_4_), channel_id=1, source_target_pairs={{0,16},{1,5},{4,20},{5,9},{8,24},{9,13},{12,28},{13,1},{16,32},{17... | collective-permute-start | bytes 786440 | tf_op jit(solution)/shard_map/ppermute | solution.py:37
  23.7 9.4 %collective-permute-start.5 = (bf16[2,32,2048]{2,1,0:T(8,128)(2,1)S(1)}, bf16[2,32,2048]{2,1,0:T(8,128)(2,1)S(1)}, u32[]{:S(2)}, u32[]{:S(2)}) collective-permute-start(bf16[2,32,2048]{2,1,0:T(8,128)(2,1)S(1)} %pad_maximum_fusion.2.refs_4_), channel_id=1, source_target_pairs={{0,48},{1,13},{4,52},{5,1},{8,56},{9,5},{12,60},{13,9},{16,0},{17,... | collective-permute-start | bytes 786440 | tf_op jit(solution)/shard_map/ppermute | solution.py:37
  25.2 9.4 %collective-permute-start.8 = (bf16[2,32,2048]{2,1,0:T(8,128)(2,1)S(1)}, bf16[2,32,2048]{2,1,0:T(8,128)(2,1)S(1)}, u32[]{:S(2)}, u32[]{:S(2)}) collective-permute-start(bf16[2,32,2048]{2,1,0:T(8,128)(2,1)S(1)} %pad_maximum_fusion.2.refs_4_), channel_id=1, source_target_pairs={{0,4},{1,17},{4,8},{5,21},{8,12},{9,25},{12,0},{13,29},{16,20},{17... | collective-permute-start | bytes 786440 | tf_op jit(solution)/shard_map/ppermute | solution.py:37
  26.9 36.4 %collective-permute-start = (bf16[2,208,1024]{2,1,0:T(8,128)(2,1)S(1)}, bf16[2,208,1024]{2,1,0:T(8,128)(2,1)S(1)}, u32[]{:S(2)}, u32[]{:S(2)}) collective-permute-start(bf16[2,208,1024]{2,1,0:T(8,128)(2,1)S(1)} %pad_maximum_fusion.refs_1_), channel_id=1, source_target_pairs={{0,1},{1,0},{4,5},{5,4},{8,9},{9,8},{12,13},{13,12},{16,17},{17,16... | collective-permute-start | bytes 2555912 | tf_op jit(solution)/shard_map/ppermute | solution.py:37
  29.2 7.4 %collective-permute-start.13 = (bf16[2,32,2048]{2,1,0:T(8,128)(2,1)S(1)}, bf16[2,32,2048]{2,1,0:T(8,128)(2,1)S(1)}, u32[]{:S(2)}, u32[]{:S(2)}) collective-permute-start(bf16[2,32,2048]{2,1,0:T(8,128)(2,1)S(1)} %pad_maximum_fusion.2.refs_4_), channel_id=1, source_target_pairs={{0,12},{1,49},{4,0},{5,53},{8,4},{9,57},{12,8},{13,61},{16,28},{17... | collective-permute-start | bytes 786440 | tf_op jit(solution)/shard_map/ppermute | solution.py:37
  33.0 11.1 %collective-permute-start.9 = (bf16[2,32,2048]{2,1,0:T(8,128)(2,1)S(1)}, bf16[2,32,2048]{2,1,0:T(8,128)(2,1)}, u32[]{:S(2)}, u32[]{:S(2)}) collective-permute-start(bf16[2,32,2048]{2,1,0:T(8,128)(2,1)S(1)} %collective-permute-done.4.refs_5_), channel_id=1, source_target_pairs={{0,4},{1,17},{4,8},{5,21},{8,12},{9,25},{12,0},{13,29},{16,20},{17... | collective-permute-start | bytes 786440 | tf_op jit(solution)/shard_map/ppermute | solution.py:37
  34.6 5.1 %collective-permute-start.6 = (bf16[1,32,2048]{2,1,0:T(8,128)(2,1)S(1)}, bf16[1,32,2048]{2,1,0:T(8,128)(2,1)S(1)}, u32[]{:S(2)}, u32[]{:S(2)}) collective-permute-start(bf16[1,32,2048]{2,1,0:T(8,128)(2,1)S(1)} %slice.83), channel_id=1, source_target_pairs={{0,16},{1,5},{4,20},{5,9},{8,24},{9,13},{12,28},{13,1},{16,32},{17... | collective-permute-start | bytes 393224 | tf_op jit(solution)/shard_map/ppermute | solution.py:37
  36.6 4.6 %collective-permute-start.7 = (bf16[1,32,2048]{2,1,0:T(8,128)(2,1)S(1)}, bf16[1,32,2048]{2,1,0:T(8,128)(2,1)}, u32[]{:S(2)}, u32[]{:S(2)}) collective-permute-start(bf16[1,32,2048]{2,1,0:T(8,128)(2,1)S(1)} %slice.84), channel_id=1, source_target_pairs={{0,48},{1,13},{4,52},{5,1},{8,56},{9,5},{12,60},{13,9},{16,0},{17,... | collective-permute-start | bytes 393224 | tf_op jit(solution)/shard_map/ppermute | solution.py:37
  39.8 6.4 %collective-permute-start.10 = (bf16[2,32,2048]{2,1,0:T(8,128)(2,1)S(1)}, bf16[2,32,2048]{2,1,0:T(8,128)(2,1)S(1)}, u32[]{:S(2)}, u32[]{:S(2)}) collective-permute-start(bf16[2,32,2048]{2,1,0:T(8,128)(2,1)S(1)} %collective-permute-done.5.refs_6_), channel_id=1, source_target_pairs={{0,4},{1,17},{4,8},{5,21},{8,12},{9,25},{12,0},{13,29},{16,20},{17... | collective-permute-start | bytes 786440 | tf_op jit(solution)/shard_map/ppermute | solution.py:37
  41.2 9.0 %collective-permute-start.14 = (bf16[2,32,2048]{2,1,0:T(8,128)(2,1)S(1)}, bf16[2,32,2048]{2,1,0:T(8,128)(2,1)S(1)}, u32[]{:S(2)}, u32[]{:S(2)}) collective-permute-start(bf16[2,32,2048]{2,1,0:T(8,128)(2,1)S(1)} %collective-permute-done.4.refs_5_), channel_id=1, source_target_pairs={{0,12},{1,49},{4,0},{5,53},{8,4},{9,57},{12,8},{13,61},{16,28},{17... | collective-permute-start | bytes 786440 | tf_op jit(solution)/shard_map/ppermute | solution.py:37
  44.1 10.2 %collective-permute-start.15 = (bf16[2,32,2048]{2,1,0:T(8,128)(2,1)S(1)}, bf16[2,32,2048]{2,1,0:T(8,128)(2,1)}, u32[]{:S(2)}, u32[]{:S(2)}) collective-permute-start(bf16[2,32,2048]{2,1,0:T(8,128)(2,1)S(1)} %collective-permute-done.5.refs_6_), channel_id=1, source_target_pairs={{0,12},{1,49},{4,0},{5,53},{8,4},{9,57},{12,8},{13,61},{16,28},{17... | collective-permute-start | bytes 786440 | tf_op jit(solution)/shard_map/ppermute | solution.py:37
  44.1 13.7 %collective-permute-start.18 = (bf16[2,32,2048]{2,1,0:T(8,128)(2,1)S(1)}, bf16[2,32,2048]{2,1,0:T(8,128)(2,1)S(1)}, u32[]{:S(2)}, u32[]{:S(2)}) collective-permute-start(bf16[2,32,2048]{2,1,0:T(8,128)(2,1)S(1)} %collective-permute-done.8.refs_9_), channel_id=1, source_target_pairs={{0,4},{1,17},{4,8},{5,21},{8,12},{9,25},{12,0},{13,29},{16,20},{17... | collective-permute-start | bytes 786440 | tf_op jit(solution)/shard_map/ppermute | solution.py:37
  46.2 11.6 %collective-permute-start.11 = (bf16[1,32,2048]{2,1,0:T(8,128)(2,1)S(1)}, bf16[1,32,2048]{2,1,0:T(8,128)(2,1)S(1)}, u32[]{:S(2)}, u32[]{:S(2)}) collective-permute-start(bf16[1,32,2048]{2,1,0:T(8,128)(2,1)S(1)} %collective-permute-done.6.refs_7_), channel_id=1, source_target_pairs={{0,4},{1,17},{4,8},{5,21},{8,12},{9,25},{12,0},{13,29},{16,20},{17... | collective-permute-start | bytes 393224 | tf_op jit(solution)/shard_map/ppermute | solution.py:37
  50.1 10.4 %collective-permute-start.16 = (bf16[1,32,2048]{2,1,0:T(8,128)(2,1)S(1)}, bf16[1,32,2048]{2,1,0:T(8,128)(2,1)}, u32[]{:S(2)}, u32[]{:S(2)}) collective-permute-start(bf16[1,32,2048]{2,1,0:T(8,128)(2,1)S(1)} %collective-permute-done.6.refs_7_), channel_id=1, source_target_pairs={{0,12},{1,49},{4,0},{5,53},{8,4},{9,57},{12,8},{13,61},{16,28},{17... | collective-permute-start | bytes 393224 | tf_op jit(solution)/shard_map/ppermute | solution.py:37
  54.3 6.2 %collective-permute-start.17 = (bf16[1,32,2048]{2,1,0:T(8,128)(2,1)}, bf16[1,32,2048]{2,1,0:T(8,128)(2,1)}, u32[]{:S(2)}, u32[]{:S(2)}) collective-permute-start(bf16[1,32,2048]{2,1,0:T(8,128)(2,1)} %collective-permute-done.7.refs_8_), channel_id=1, source_target_pairs={{0,12},{1,49},{4,0},{5,53},{8,4},{9,57},{12,8},{13,61},{16,28},{17... | collective-permute-start | bytes 393224 | tf_op jit(solution)/shard_map/ppermute | solution.py:37
  57.8 11.2 %collective-permute-start.19 = (bf16[2,32,2048]{2,1,0:T(8,128)(2,1)}, bf16[2,32,2048]{2,1,0:T(8,128)(2,1)}, u32[]{:S(2)}, u32[]{:S(2)}) collective-permute-start(bf16[2,32,2048]{2,1,0:T(8,128)(2,1)} %collective-permute-done.9.refs_10_), channel_id=1, source_target_pairs={{0,4},{1,17},{4,8},{5,21},{8,12},{9,25},{12,0},{13,29},{16,20},{17... | collective-permute-start | bytes 786440 | tf_op jit(solution)/shard_map/ppermute | solution.py:37
  57.9 11.2 %collective-permute-start.20 = (bf16[2,32,2048]{2,1,0:T(8,128)(2,1)}, bf16[2,32,2048]{2,1,0:T(8,128)(2,1)}, u32[]{:S(2)}, u32[]{:S(2)}) collective-permute-start(bf16[2,32,2048]{2,1,0:T(8,128)(2,1)} %collective-permute-done.15.refs_16_), channel_id=1, source_target_pairs={{0,12},{1,49},{4,0},{5,53},{8,4},{9,57},{12,8},{13,61},{16,28},{17... | collective-permute-start | bytes 786440 | tf_op jit(solution)/shard_map/ppermute | solution.py:37
  60.5 5.5 %collective-permute-start.12 = (bf16[1,32,2048]{2,1,0:T(8,128)(2,1)}, bf16[1,32,2048]{2,1,0:T(8,128)(2,1)}, u32[]{:S(2)}, u32[]{:S(2)}) collective-permute-start(bf16[1,32,2048]{2,1,0:T(8,128)(2,1)} %collective-permute-done.7.refs_8_), channel_id=1, source_target_pairs={{0,4},{1,17},{4,8},{5,21},{8,12},{9,25},{12,0},{13,29},{16,20},{17... | collective-permute-start | bytes 393224 | tf_op jit(solution)/shard_map/ppermute | solution.py:37
  60.5 5.5 %collective-permute-start.21 = (bf16[1,32,2048]{2,1,0:T(8,128)(2,1)}, bf16[1,32,2048]{2,1,0:T(8,128)(2,1)}, u32[]{:S(2)}, u32[]{:S(2)}) collective-permute-start(bf16[1,32,2048]{2,1,0:T(8,128)(2,1)} %collective-permute-done.16.refs_17_), channel_id=1, source_target_pairs={{0,12},{1,49},{4,0},{5,53},{8,4},{9,57},{12,8},{13,61},{16,28},{17... | collective-permute-start | bytes 393224 | tf_op jit(solution)/shard_map/ppermute | solution.py:37
  63.4 5.6 %collective-permute-start.22 = (bf16[1,32,2048]{2,1,0:T(8,128)(2,1)}, bf16[1,32,2048]{2,1,0:T(8,128)(2,1)}, u32[]{:S(2)}, u32[]{:S(2)}) collective-permute-start(bf16[1,32,2048]{2,1,0:T(8,128)(2,1)} %collective-permute-done.17.refs_18_), channel_id=1, source_target_pairs={{0,12},{1,49},{4,0},{5,53},{8,4},{9,57},{12,8},{13,61},{16,28},{17... | collective-permute-start | bytes 393224 | tf_op jit(solution)/shard_map/ppermute | solution.py:37
  104.7 20.8 %collective-permute-start.31 = (bf16[144,2048]{1,0:T(8,128)(2,1)}, bf16[144,2048]{1,0:T(8,128)(2,1)S(1)}, u32[]{:S(2)}, u32[]{:S(2)}) collective-permute-start(bf16[144,2048]{1,0:T(8,128)(2,1)} %get-tuple-element.71), channel_id=1, source_target_pairs={{0,4},{1,17},{4,8},{5,21},{8,12},{9,25},{12,0},{13,29},{16,20},{17... | collective-permute-start | bytes 1769480 | tf_op jit(solution)/shard_map/ppermute | solution.py:37
  105.4 15.2 %collective-permute-start.25 = (bf16[128,2048]{1,0:T(8,128)(2,1)}, bf16[128,2048]{1,0:T(8,128)(2,1)S(1)}, u32[]{:S(2)}, u32[]{:S(2)}) collective-permute-start(bf16[128,2048]{1,0:T(8,128)(2,1)} %get-tuple-element.62), channel_id=1, source_target_pairs={{0,4},{1,17},{4,8},{5,21},{8,12},{9,25},{12,0},{13,29},{16,20},{17... | collective-permute-start | bytes 1572872 | tf_op jit(solution)/shard_map/ppermute | solution.py:37
  106.9 15.1 %collective-permute-start.26 = (bf16[128,2048]{1,0:T(8,128)(2,1)}, bf16[128,2048]{1,0:T(8,128)(2,1)S(1)}, u32[]{:S(2)}, u32[]{:S(2)}) collective-permute-start(bf16[128,2048]{1,0:T(8,128)(2,1)} %get-tuple-element.63), channel_id=1, source_target_pairs={{0,12},{1,49},{4,0},{5,53},{8,4},{9,57},{12,8},{13,61},{16,28},{17... | collective-permute-start | bytes 1572872 | tf_op jit(solution)/shard_map/ppermute | solution.py:37
  108.1 20.2 %collective-permute-start.32 = (bf16[144,2048]{1,0:T(8,128)(2,1)}, bf16[144,2048]{1,0:T(8,128)(2,1)S(1)}, u32[]{:S(2)}, u32[]{:S(2)}) collective-permute-start(bf16[144,2048]{1,0:T(8,128)(2,1)} %get-tuple-element.72), channel_id=1, source_target_pairs={{0,12},{1,49},{4,0},{5,53},{8,4},{9,57},{12,8},{13,61},{16,28},{17... | collective-permute-start | bytes 1769480 | tf_op jit(solution)/shard_map/ppermute | solution.py:37
  109.0 40.9 %collective-permute-start.28 = (bf16[128,2048]{1,0:T(8,128)(2,1)}, bf16[128,2048]{1,0:T(8,128)(2,1)}, u32[]{:S(2)}, u32[]{:S(2)}) collective-permute-start(bf16[128,2048]{1,0:T(8,128)(2,1)} %get-tuple-element.65), channel_id=1, source_target_pairs={{0,4},{1,17},{4,8},{5,21},{8,12},{9,25},{12,0},{13,29},{16,20},{17... | collective-permute-start | bytes 1572872 | tf_op jit(solution)/shard_map/ppermute | solution.py:37
  120.6 29.4 %collective-permute-start.29 = (bf16[128,2048]{1,0:T(8,128)(2,1)}, bf16[128,2048]{1,0:T(8,128)(2,1)}, u32[]{:S(2)}, u32[]{:S(2)}) collective-permute-start(bf16[128,2048]{1,0:T(8,128)(2,1)} %get-tuple-element.66), channel_id=1, source_target_pairs={{0,12},{1,49},{4,0},{5,53},{8,4},{9,57},{12,8},{13,61},{16,28},{17... | collective-permute-start | bytes 1572872 | tf_op jit(solution)/shard_map/ppermute | solution.py:37
  125.6 25.7 %collective-permute-start.27 = (bf16[128,2048]{1,0:T(8,128)(2,1)}, bf16[128,2048]{1,0:T(8,128)(2,1)S(1)}, u32[]{:S(2)}, u32[]{:S(2)}) collective-permute-start(bf16[128,2048]{1,0:T(8,128)(2,1)} %get-tuple-element.64), channel_id=1, source_target_pairs={{0,4},{1,17},{4,8},{5,21},{8,12},{9,25},{12,0},{13,29},{16,20},{17... | collective-permute-start | bytes 1572872 | tf_op jit(solution)/shard_map/ppermute | solution.py:37
  125.6 27.2 %collective-permute-start.30 = (bf16[128,2048]{1,0:T(8,128)(2,1)}, bf16[128,2048]{1,0:T(8,128)(2,1)}, u32[]{:S(2)}, u32[]{:S(2)}) collective-permute-start(bf16[128,2048]{1,0:T(8,128)(2,1)} %get-tuple-element.67), channel_id=1, source_target_pairs={{0,12},{1,49},{4,0},{5,53},{8,4},{9,57},{12,8},{13,61},{16,28},{17... | collective-permute-start | bytes 1572872 | tf_op jit(solution)/shard_map/ppermute | solution.py:37
  128.2 46.2 %collective-permute-start.23 = (f32[208,1024]{1,0:T(8,128)}, f32[208,1024]{1,0:T(8,128)S(1)}, u32[]{:S(2)}, u32[]{:S(2)}) collective-permute-start(f32[208,1024]{1,0:T(8,128)} %get-tuple-element.54), channel_id=1, source_target_pairs={{0,1},{1,0},{4,5},{5,4},{8,9},{9,8},{12,13},{13,12},{16,17},{17,16... | collective-permute-start | bytes 2555912 | tf_op jit(solution)/shard_map/ppermute | solution.py:37
  149.9 16.3 %collective-permute-start.33 = (bf16[144,2048]{1,0:T(8,128)(2,1)}, bf16[144,2048]{1,0:T(8,128)(2,1)S(1)}, u32[]{:S(2)}, u32[]{:S(2)}) collective-permute-start(bf16[144,2048]{1,0:T(8,128)(2,1)} %get-tuple-element.73), channel_id=1, source_target_pairs={{0,4},{1,17},{4,8},{5,21},{8,12},{9,25},{12,0},{13,29},{16,20},{17... | collective-permute-start | bytes 1769480 | tf_op jit(solution)/shard_map/ppermute | solution.py:37
  150.0 16.1 %collective-permute-start.34 = (bf16[128,2048]{1,0:T(8,128)(2,1)}, bf16[128,2048]{1,0:T(8,128)(2,1)}, u32[]{:S(2)}, u32[]{:S(2)}) collective-permute-start(bf16[128,2048]{1,0:T(8,128)(2,1)} %get-tuple-element.74), channel_id=1, source_target_pairs={{0,4},{1,17},{4,8},{5,21},{8,12},{9,25},{12,0},{13,29},{16,20},{17... | collective-permute-start | bytes 1572872 | tf_op jit(solution)/shard_map/ppermute | solution.py:37
  151.3 14.9 %collective-permute-start.35 = (bf16[128,2048]{1,0:T(8,128)(2,1)}, bf16[128,2048]{1,0:T(8,128)(2,1)}, u32[]{:S(2)}, u32[]{:S(2)}) collective-permute-start(bf16[128,2048]{1,0:T(8,128)(2,1)} %get-tuple-element.75), channel_id=1, source_target_pairs={{0,12},{1,49},{4,0},{5,53},{8,4},{9,57},{12,8},{13,61},{16,28},{17... | collective-permute-start | bytes 1572872 | tf_op jit(solution)/shard_map/ppermute | solution.py:37
  152.7 13.4 %collective-permute-start.36 = (bf16[128,2048]{1,0:T(8,128)(2,1)}, bf16[128,2048]{1,0:T(8,128)(2,1)}, u32[]{:S(2)}, u32[]{:S(2)}) collective-permute-start(bf16[128,2048]{1,0:T(8,128)(2,1)} %get-tuple-element.76), channel_id=1, source_target_pairs={{0,12},{1,49},{4,0},{5,53},{8,4},{9,57},{12,8},{13,61},{16,28},{17... | collective-permute-start | bytes 1572872 | tf_op jit(solution)/shard_map/ppermute | solution.py:37
  171.2 8.2 %collective-permute-start.37 = (bf16[80,2048]{1,0:T(8,128)(2,1)}, bf16[80,2048]{1,0:T(8,128)(2,1)}, u32[]{:S(2)}, u32[]{:S(2)}) collective-permute-start(bf16[80,2048]{1,0:T(8,128)(2,1)} %get-tuple-element.82), channel_id=1, source_target_pairs={{0,16},{1,5},{4,20},{5,9},{8,24},{9,13},{12,28},{13,1},{16,32},{17... | collective-permute-start | bytes 983048 | tf_op jit(solution)/shard_map/ppermute | solution.py:37
  171.2 8.2 %collective-permute-start.38 = (bf16[80,2048]{1,0:T(8,128)(2,1)}, bf16[80,2048]{1,0:T(8,128)(2,1)}, u32[]{:S(2)}, u32[]{:S(2)}) collective-permute-start(bf16[80,2048]{1,0:T(8,128)(2,1)} %get-tuple-element.83), channel_id=1, source_target_pairs={{0,48},{1,13},{4,52},{5,1},{8,56},{9,5},{12,60},{13,9},{16,0},{17,... | collective-permute-start | bytes 983048 | tf_op jit(solution)/shard_map/ppermute | solution.py:37
  175.4 24.2 %collective-permute-start.24 = (f32[144,1024]{1,0:T(8,128)}, f32[144,1024]{1,0:T(8,128)S(1)}, u32[]{:S(2)}, u32[]{:S(2)}) collective-permute-start(f32[144,1024]{1,0:T(8,128)} %get-tuple-element.58), channel_id=1, source_target_pairs={{0,1},{1,0},{4,5},{5,4},{8,9},{9,8},{12,13},{13,12},{16,17},{17,16... | collective-permute-start | bytes 1769480 | tf_op jit(solution)/shard_map/ppermute | solution.py:37
  181.9 10.6 %collective-permute-start.39 = (bf16[144,2048]{1,0:T(8,128)(2,1)}, bf16[144,2048]{1,0:T(8,128)(2,1)}, u32[]{:S(2)}, u32[]{:S(2)}) collective-permute-start(bf16[144,2048]{1,0:T(8,128)(2,1)} %get-tuple-element.84), channel_id=1, source_target_pairs={{0,16},{1,5},{4,20},{5,9},{8,24},{9,13},{12,28},{13,1},{16,32},{17... | collective-permute-start | bytes 1769480 | tf_op jit(solution)/shard_map/ppermute | solution.py:37
  182.6 9.1 %collective-permute-start.40 = (bf16[128,2048]{1,0:T(8,128)(2,1)}, bf16[128,2048]{1,0:T(8,128)(2,1)}, u32[]{:S(2)}, u32[]{:S(2)}) collective-permute-start(bf16[128,2048]{1,0:T(8,128)(2,1)} %get-tuple-element.85), channel_id=1, source_target_pairs={{0,48},{1,13},{4,52},{5,1},{8,56},{9,5},{12,60},{13,9},{16,0},{17,... | collective-permute-start | bytes 1572872 | tf_op jit(solution)/shard_map/ppermute | solution.py:37
  195.4 8.2 %collective-permute-start.41 = (bf16[72,2560]{1,0:T(8,128)(2,1)}, bf16[72,2560]{1,0:T(8,128)(2,1)S(1)}, u32[]{:S(2)}, u32[]{:S(2)}) collective-permute-start(bf16[72,2560]{1,0:T(8,128)(2,1)} %get-tuple-element.87), channel_id=1, source_target_pairs={{0,64},{1,65},{4,68},{5,69},{8,72},{9,73},{12,76},{13,77},{16,80},... | collective-permute-start | bytes 1105928 | tf_op jit(solution)/shard_map/ppermute | solution.py:37
  197.2 6.6 %collective-permute-start.42 = (bf16[72,2560]{1,0:T(8,128)(2,1)}, bf16[72,2560]{1,0:T(8,128)(2,1)S(1)}, u32[]{:S(2)}, u32[]{:S(2)}) collective-permute-start(bf16[72,2560]{1,0:T(8,128)(2,1)} %get-tuple-element.87), channel_id=1, source_target_pairs={{0,66},{1,67},{4,70},{5,71},{8,74},{9,75},{12,78},{13,79},{16,82},... | collective-permute-start | bytes 1105928 | tf_op jit(solution)/shard_map/ppermute | solution.py:37
  198.4 13.1 %collective-permute-start.43 = (bf16[72,2560]{1,0:T(8,128)(2,1)}, bf16[72,2560]{1,0:T(8,128)(2,1)S(1)}, u32[]{:S(2)}, u32[]{:S(2)}) collective-permute-start(bf16[72,2560]{1,0:T(8,128)(2,1)} %get-tuple-element.86.same), channel_id=1, source_target_pairs={{0,2},{1,3},{4,6},{5,7},{8,10},{9,11},{12,14},{13,15},{16,18},{17,... | collective-permute-start | bytes 1105928 | tf_op jit(solution)/shard_map/ppermute | solution.py:37
  214.6 9.2 %collective-permute-start.44 = (f32[72,2560]{1,0:T(8,128)}, f32[72,2560]{1,0:T(8,128)S(1)}, u32[]{:S(2)}, u32[]{:S(2)}) collective-permute-start(f32[72,2560]{1,0:T(8,128)} %shard_map.193.mine), channel_id=1, source_target_pairs={{0,1},{1,0},{4,5},{5,4},{8,9},{9,8},{12,13},{13,12},{16,17},{17,16... | collective-permute-start | bytes 2211848 | tf_op jit(solution)/shard_map/ppermute | solution.py:37
  (34 other events, 661.7 us)
Sparse Core Ops, SparseCore 0:
  10.9 77.0 all-gather.1

commit v2 on v1

--- a/solution.py
+++ b/solution.py
@@ -58,7 +58,8 @@
 
 
 def coordinates():
-    return jnp.stack([lax.axis_index(name) for name in ("fsdp_1", "fsdp_2", "rep_1", "fsdp_0")]).astype(jnp.int32)
+    names = ("fsdp_1", "fsdp_2", "rep_1", "fsdp_0", "rep_0")
+    return jnp.stack([lax.axis_index(name) for name in names]).astype(jnp.int32)
 
 
 def block_row(where, block):
@@ -92,7 +93,7 @@
 
 def local_body(length, placed, where, own, peer, gain, *refs):
     size = own.shape[1]
-    n_weights = 2 if placed else 20
+    n_weights = 2 if placed else 16
     weights, refs = refs[:n_weights], refs[n_weights:]
     grads, refs = refs[:7], refs[7:]
     dh, gain_part, refs = refs[:2], refs[2], refs[3:]
@@ -217,10 +218,7 @@
     return (rows[0:1] + rows[1:2]) + rows[2:3]
 
 
-PIECE_BLOCKS = []
-for start in (0, 8, 16):
-    PIECE_BLOCKS += [(start, start + 1), (start + 2, start + 3), (start + 4, start + 5), (start + 6,), (start + 7,)]
-PIECE_BLOCKS += [(24, 25), (26, 27), (28, 29), (30,), (31,)]
+PIECE_BLOCKS = [(n, n + 1) for n in range(0, 32, 2)]
 GRAD_BLOCKS = [tuple(range(8))]
 for start in (8, 16, 24):
     GRAD_BLOCKS += [tuple(range(start, start + 4)), tuple(range(start + 4, start + 8))]
@@ -258,26 +256,28 @@
     )(where, own, peer, gain.reshape(1, 1024), *weights)
 
 
-def my_columns(qkv_shard):
-    c = lax.axis_index("rep_1")
-    halves = qkv_shard.reshape(32, 3, 2, 512)
-    return jnp.where(c == 0, halves[:, :, 0], halves[:, :, 1]).reshape(32, 1536)
-
-
-def gather_by_calls(qkv_shard, out_shard):
-    high = lax.axis_index("rep_0")
-    shard = jnp.concatenate([my_columns(qkv_shard), out_shard], 1)
-    shard = jnp.where(high == 0, shard[:, :1280], shard[:, 1280:])
-    return lax.all_gather(shard, ("rep_0",) + FSDP, axis=0, tiled=True)
-
-
-def gather_by_rings(qkv_shard, out_shard):
+def prepare(where, v_qkv, v_out, a_qkv, a_out, top, bottom, part):
+    c, high = where[2], where[4]
+    for k in range(3):
+        at = pl.multiple_of(1024 * k + 512 * c, 512)
+        top[:, 512 * k : 512 * k + 512] = v_qkv[:16, pl.ds(at, 512)]
+        bottom[:, 512 * k : 512 * k + 512] = v_qkv[16:, pl.ds(at, 512)]
+    top[:, 1536:] = v_out[:16, :]
+    bottom[:, 1536:] = v_out[16:, :]
+    flip = jnp.full((32, 1280), high, jnp.int32) == 1
+    parts = [a_qkv[:, pl.ds(pl.multiple_of(1024 * k + 512 * c, 512), 512)] for k in range(3)]
+    first = jnp.concatenate([parts[0], parts[1], parts[2][:, :256]], 1).astype(f32)
+    second = jnp.concatenate([parts[2][:, 256:], a_out[...]], 1).astype(f32)
+    part[...] = jnp.where(flip, second, first).astype(bf16)
+
+
+def gather_by_rings(top, bottom):
     low = lax.axis_index("fsdp_0")
     c = lax.axis_index("rep_1")
-    shard = jnp.concatenate([my_columns(qkv_shard), out_shard], 1)
-    top = send(shard[:16], along_y(1))
-    bottom = send(shard[16:], along_y(-1))
-    other = jnp.concatenate([top, bottom], 0)
+    other_top = send(top, along_y(1))
+    other_bottom = send(bottom, along_y(-1))
+    shard = jnp.concatenate([top, bottom], 0)
+    other = jnp.concatenate([other_top, other_bottom], 0)
     first = jnp.where(low == 0, shard[:, :1536], other[:, :1536])
     second = jnp.where(low == 0, other[:, :1536], shard[:, :1536])
     outw = jnp.where(low == c, shard[:, 1536:], other[:, 1536:])
@@ -289,9 +289,8 @@
     )
     left = send(block, along_mid(1))
     right = send(block, along_mid(-1))
-    far_a = send(left[:1], along_mid(1))
-    far_b = send(right[1:], along_mid(-1))
-    own = [block, left, right, far_a, far_b]
+    far = send(left, along_mid(1))
+    own = [block, left, right, far]
     from_left = [send(piece, along_last(1)) for piece in own]
     from_right = [send(piece, along_last(-1)) for piece in own]
     across = [send(piece, along_last(1)) for piece in from_left[:2]]
@@ -355,7 +354,7 @@
 
 
 def fold_last(video, own, up_a, up_b, down_a, down_b, gain, up_far, down_far,
-              far_up, far_down, right, left, home, gain_out):
+              right, left, across, home, gain_out):
     for s in range(2):
         for j in range(8):
             u, d, at = (up_a, down_a, 32 * j) if j < 4 else (up_b, down_b, 32 * j - 128)
@@ -363,13 +362,8 @@
                 total = video[32 * j : 32 * j + 32, :].astype(f32)
             else:
                 total = add(own[32 * j : 32 * j + 32, :], u[at : at + 32, :], d[at : at + 32, :])
-            if j < 2:
-                home[64 * s + 32 * j : 64 * s + 32 * j + 32, :] = total
-            elif j < 6:
-                row = 64 * s + 32 * (j % 2)
-                (left if j < 4 else right)[row : row + 32, :] = total.astype(bf16)
-            else:
-                (far_up if j == 6 else far_down)[32 * s : 32 * s + 32, :] = total.astype(bf16)
+            row = 64 * s + 32 * (j % 2)
+            (home, left, right, across)[j // 2][row : row + 32, :] = total.astype(bf16)
     total = ring_sum(
         gain[...],
         from_pieces(up_far[128:144, :]),
@@ -377,25 +371,15 @@
         from_pieces(up_a[128:144, :]),
     )
     gain_out[...] = total
-    far_up[64:80, :] = in_pieces(total)
-    far_down[64:80, :] = in_pieces(total)
-
-
-def fold_mid_far(right, left, up, down, right_out, left_out):
-    for s in range(2):
-        a, b, c = 64 * s, 64 * s + 32, 64 * s + 64
-        right_out[a:b, :] = add(right[a:b, :], up[32 * s : 32 * s + 32, :]).astype(bf16)
-        right_out[b:c, :] = right[b:c, :]
-        left_out[a:b, :] = left[a:b, :]
-        left_out[b:c, :] = add(left[b:c, :], down[32 * s : 32 * s + 32, :]).astype(bf16)
-    right_out[128:144, :] = up[64:80, :]
-
-
-def fold_mid(where, home, gain, up, down, up_far, down_far, same, cross, gain_out):
+    for ref in (right, left, across):
+        ref[128:144, :] = in_pieces(total)
+
+
+def fold_mid(where, home, gain, up, down, far, same, cross, gain_out):
     low = where[3]
     for s in range(2):
         first, second = (
-            add(home[r, :], up[r, :], down[r, :]).astype(bf16)
+            add(home[r, :], far[r, :], up[r, :], down[r, :]).astype(bf16)
             for r in (pl.ds(64 * s, 32), pl.ds(64 * s + 32, 32))
         )
         r = slice(32 * s, 32 * s + 32)
@@ -408,9 +392,9 @@
             ref[r, 2048:] = second[:, 1536:]
     total = ring_sum(
         gain[...],
-        from_pieces(up_far[64:80, :]),
-        from_pieces(down_far[64:80, :]),
         from_pieces(up[128:144, :]),
+        from_pieces(down[128:144, :]),
+        from_pieces(far[128:144, :]),
     )
     gain_out[...] = total
     for ref in (same, cross):
@@ -450,21 +434,15 @@
 def last_steps(video, audio, audio_parts, gain, where, count):
     audio_far = audio_parts[3:5]
     (video_sum,) = in_one_kernel(fold_sum, [((256, 2048), bf16)], *video)
-    far_up, far_down, right, left, home, gain = in_one_kernel(
+    right, left, across, home, gain = in_one_kernel(
         fold_last,
-        [((80, 2048), bf16)] * 2
-        + [((128, 2048), bf16)] * 2
-        + [((128, 2048), f32), ((1, 2048), f32)],
+        [((144, 2048), bf16)] * 3 + [((128, 2048), bf16), ((1, 2048), f32)],
         video_sum,
         *audio,
         gain,
         *audio_far,
     )
-    up_far = send(far_up, along_mid(1))
-    down_far = send(far_down, along_mid(-1))
-    right, left = in_one_kernel(
-        fold_mid_far, [((144, 2048), bf16), ((128, 2048), bf16)], right, left, up_far, down_far
-    )
+    far = send(across, along_mid(2))
     up = send(right, along_mid(1))
     down = send(left, along_mid(-1))
     same, cross, gain = in_one_kernel(
@@ -474,8 +452,7 @@
         gain,
         up,
         down,
-        up_far,
-        down_far,
+        far,
         scalars=where,
     )
     far = send(same, along_y(2))
@@ -534,8 +511,17 @@
     video_len = video_in.shape[1]
     audio_len = audio_in.shape[1]
     bottle_len = bottle_in.shape[1]
-    aweights = gather_by_calls(audio_qkv, audio_out)
-    vweights = gather_by_rings(video_qkv, video_out)
+    top, bottom, part = in_one_kernel(
+        prepare,
+        [((16, 2560), bf16)] * 2 + [((32, 1280), bf16)],
+        video_qkv,
+        video_out,
+        audio_qkv,
+        audio_out,
+        scalars=where,
+    )
+    aweights = lax.all_gather(part, ("rep_0",) + FSDP, axis=0, tiled=True)
+    vweights = gather_by_rings(top, bottom)
     vown, vpeer = clip_pair(video_in[0], bottle_in[0], grad_video[0], grad_bottle[0])
     aown, apeer = clip_pair(audio_in[0], bottle_in[0], grad_audio[0], grad_bottle[0])
     vpeer, apeer = lax.optimization_barrier((vpeer, apeer))

time: 235 us -> 212 us (0.902)
  starting transfers between devices: 86.3 us -> 57.4 us
  waiting for transfers between devices: 53.9 us -> 60.2 us
    ppermute x45 -> x40, starting transfers between devices: 86.2 us -> 57.4 us  [send(): return lax.ppermute(value, FSDP_REP, pairs(move))]
    all_gather x1, waiting for transfers between devices: 1.53 us -> 4.91 us  [per_device(): aweights = lax.all_gather(part, ('rep_0',) + FSDP, axis=0, tiled=True)]
    ppermute x45 -> x40, waiting for transfers between devices: 52.4 us -> 55.2 us  [send(): return lax.ppermute(value, FSDP_REP, pairs(move))]
    unnamed x76 -> x92, local copies, waits for them, and re-layouts: 4.37 us -> 6.54 us
  transfers between devices with their start and end apart: 46 -> 41, of which waited for: 18 -> 19; matrix products, arithmetic and copies ran while one was open for 6% -> 7% of each run, Pallas kernels for 15% -> 16%
where the time goes in v2:
time: 212 us; the launch traced here: 211 us
  waiting for transfers between devices  60.2 us (28%)
  starting transfers between devices  57.4 us (27%)
  Pallas kernels  56.1 us (26%)
  between operations  14.4 us (7%)
  other arithmetic  13.8 us (7%)
  local copies, waits for them, and re-layouts  8.88 us (4%)
    ppermute x40, starting transfers between devices, send(): return lax.ppermute(value, FSDP_REP, pairs(move))  57.4 us
    ppermute x40, waiting for transfers between devices, send(): return lax.ppermute(value, FSDP_REP, pairs(move))  55.2 us
    pallas_call x2, Pallas kernels, local_compute(): pl.pallas_call(lambda *refs: local_body(length, placed, *refs), in_specs=...  34.1 us
    pallas_call x8, Pallas kernels, in_one_kernel(): pl.pallas_call(body, in_specs=specs, out_specs=in_vmem(len(shapes)), out_...  22 us
    unnamed x92, local copies, waits for them, and re-layouts  6.54 us
    all_gather x1, waiting for transfers between devices, per_device(): aweights = lax.all_gather(part, ('rep_0',) + FSDP, axis=0, tiled=True)  4.91 us
  transfers between devices with their start and end apart: 41, of which 19 were waited for; matrix products, arithmetic and copies ran while one was open for 7% of the time, Pallas kernels for 16%

profile of v2, /device:TPU:1, one launch (start us, length us, event | category | flops | bytes accessed | tf_op | source)
XLA Modules:
  0.0 210.8 jit_solution(7268216371921941822)
XLA Ops:
  7.8 1.8 shard_map.187
  11.9 1.5 collective-permute-start
  15.0 1.4 collective-permute-start.2
  16.4 1.5 collective-permute-start.3
  18.0 2.2 %collective-permute-done.2 = bf16[16,2560]{1,0:T(8,128)(2,1)S(1)} collective-permute-done((bf16[16,2560]{1,0:T(8,128)(2,1)S(1)}, bf16[16,2560]{1,0:T(8,128)(2,1)S(1)}, u32[]{:S(2)}, u32[]{:S(2)}) %collective-permute-start.2) | collective-permute-done | bytes 81952 | tf_op jit(solution)/shard_map/ppermute | solution.py:37
  21.5 1.6 collective-permute-start.5
  23.1 1.5 collective-permute-start.7
  24.6 2.5 %collective-permute-done.4.refs_5_ = bf16[2,32,2048]{2,1,0:T(8,128)(2,1)S(1)} collective-permute-done((bf16[2,32,2048]{2,1,0:T(8,128)(2,1)S(1)}, bf16[2,32,2048]{2,1,0:T(8,128)(2,1)S(1)}, u32[]{:S(2)}, u32[]{:S(2)}) %collective-permute-start.4) | collective-permute-done | bytes 262176 | tf_op jit(solution)/shard_map/ppermute | solution.py:37
  27.2 3.6 %collective-permute-start.11 = (bf16[2,32,2048]{2,1,0:T(8,128)(2,1)S(1)}, bf16[2,32,2048]{2,1,0:T(8,128)(2,1)S(1)}, u32[]{:S(2)}, u32[]{:S(2)}) collective-permute-start(bf16[2,32,2048]{2,1,0:T(8,128)(2,1)S(1)} %pad_maximum_fusion.2.refs_4_), channel_id=1, source_target_pairs={{0,12},{1,49},{4,0},{5,53},{8,4},{9,57},{12,8},{13,61},{16,28},{17... | collective-permute-start | bytes 786440 | tf_op jit(solution)/shard_map/ppermute | solution.py:37
  31.1 1.7 collective-permute-done.7.refs_8_
  32.8 1.4 collective-permute-done.11.refs_12_
  34.7 2.8 %collective-permute-start.12 = (bf16[2,32,2048]{2,1,0:T(8,128)(2,1)S(1)}, bf16[2,32,2048]{2,1,0:T(8,128)(2,1)S(1)}, u32[]{:S(2)}, u32[]{:S(2)}) collective-permute-start(bf16[2,32,2048]{2,1,0:T(8,128)(2,1)S(1)} %collective-permute-done.4.refs_5_), channel_id=1, source_target_pairs={{0,12},{1,49},{4,0},{5,53},{8,4},{9,57},{12,8},{13,61},{16,28},{17... | collective-permute-start | bytes 786440 | tf_op jit(solution)/shard_map/ppermute | solution.py:37
  37.5 1.4 collective-permute-start.13
  40.4 4.6 %collective-permute-done.9.refs_10_ = bf16[2,32,2048]{2,1,0:T(8,128)(2,1)S(1)} collective-permute-done((bf16[2,32,2048]{2,1,0:T(8,128)(2,1)S(1)}, bf16[2,32,2048]{2,1,0:T(8,128)(2,1)S(1)}, u32[]{:S(2)}, u32[]{:S(2)}) %collective-permute-start.9) | collective-permute-done | bytes 262176 | tf_op jit(solution)/shard_map/ppermute | solution.py:37
  46.9 1.4 collective-permute-start.17
  48.3 2.4 %collective-permute-start.18 = (bf16[2,32,2048]{2,1,0:T(8,128)(2,1)S(1)}, bf16[2,32,2048]{2,1,0:T(8,128)(2,1)S(1)}, u32[]{:S(2)}, u32[]{:S(2)}) collective-permute-start(bf16[2,32,2048]{2,1,0:T(8,128)(2,1)S(1)} %collective-permute-done.14.refs_15_), channel_id=1, source_target_pairs={{0,12},{1,49},{4,0},{5,53},{8,4},{9,57},{12,8},{13,61},{16,28},{17... | collective-permute-start | bytes 786440 | tf_op jit(solution)/shard_map/ppermute | solution.py:37
  50.7 1.7 collective-permute-done.15.refs_16_
  52.5 4.0 %collective-permute-done.10.refs_11_ = bf16[2,32,2048]{2,1,0:T(8,128)(2,1)S(1)} collective-permute-done((bf16[2,32,2048]{2,1,0:T(8,128)(2,1)S(1)}, bf16[2,32,2048]{2,1,0:T(8,128)(2,1)S(1)}, u32[]{:S(2)}, u32[]{:S(2)}) %collective-permute-start.10) | collective-permute-done | bytes 262176 | tf_op jit(solution)/shard_map/ppermute | solution.py:37
  56.5 3.8 %collective-permute-done.16.refs_17_ = bf16[2,32,2048]{2,1,0:T(8,128)(2,1)S(1)} collective-permute-done((bf16[2,32,2048]{2,1,0:T(8,128)(2,1)S(1)}, bf16[2,32,2048]{2,1,0:T(8,128)(2,1)S(1)}, u32[]{:S(2)}, u32[]{:S(2)}) %collective-permute-start.16) | collective-permute-done | bytes 262176 | tf_op jit(solution)/shard_map/ppermute | solution.py:37
  61.9 17.3 %local_pieces.1 = (bf16[256,2048]{1,0:T(8,128)(2,1)}, bf16[128,2048]{1,0:T(8,128)(2,1)}, bf16[128,2048]{1,0:T(8,128)(2,1)}, bf16[128,2048]{1,0:T(8,128)(2,1)}, b...) custom-call(s32[5]{0:T(128)} %stack.50.where.refs_0_, ...), custom_call_target="tpu_custom_call" | custom-call | tf_op jit(solution)/shard_map/local_pieces/pallas_call | solution.py:230
  79.2 4.9 %all-gather.2.cloned.1.call-done.refs_4_ = bf16[2048,1280]{1,0:T(8,128)(2,1)} async-done(((bf16[32,1280]{1,0:T(8,128)(2,1)}), bf16[2048,1280]{1,0:T(8,128)(2,1)}) %all-gather.2.cloned.1.call-update) | async-done | bytes 5242896 | tf_op jit(solution)/shard_map/all_gather | solution.py:523
  84.2 16.8 %local_placed.1 = (bf16[256,2048]{1,0:T(8,128)(2,1)}, bf16[128,2048]{1,0:T(8,128)(2,1)}, bf16[128,2048]{1,0:T(8,128)(2,1)}, bf16[128,2048]{1,0:T(8,128)(2,1)}, b...) custom-call(s32[5]{0:T(128)} %stack.50.where.refs_0_, ...), custom_call_target="tpu_custom_call" | custom-call | tf_op jit(solution)/shard_map/local_placed/pallas_call | solution.py:230
  103.2 1.4 collective-permute-start.22
  104.6 2.2 %collective-permute-start.19 = (f32[208,1024]{1,0:T(8,128)}, f32[208,1024]{1,0:T(8,128)S(1)}, u32[]{:S(2)}, u32[]{:S(2)}) collective-permute-start(f32[208,1024]{1,0:T(8,128)} %get-tuple-element.56), channel_id=1, source_target_pairs={{0,1},{1,0},{4,5},{5,4},{8,9},{9,8},{12,13},{13,12},{16,17},{17,16... | collective-permute-start | bytes 2555912 | tf_op jit(solution)/shard_map/ppermute | solution.py:37
  108.0 9.1 %collective-permute-done.21.up = bf16[128,2048]{1,0:T(8,128)(2,1)} collective-permute-done((bf16[128,2048]{1,0:T(8,128)(2,1)}, bf16[128,2048]{1,0:T(8,128)(2,1)}, u32[]{:S(2)}, u32[]{:S(2)}) %collective-permute-start.21) | collective-permute-done | bytes 524320 | tf_op jit(solution)/shard_map/ppermute | solution.py:37
  117.1 2.7 %collective-permute-start.25 = (bf16[128,2048]{1,0:T(8,128)(2,1)}, bf16[128,2048]{1,0:T(8,128)(2,1)}, u32[]{:S(2)}, u32[]{:S(2)}) collective-permute-start(bf16[128,2048]{1,0:T(8,128)(2,1)} %get-tuple-element.69), channel_id=1, source_target_pairs={{0,12},{1,49},{4,0},{5,53},{8,4},{9,57},{12,8},{13,61},{16,28},{17... | collective-permute-start | bytes 1572872 | tf_op jit(solution)/shard_map/ppermute | solution.py:37
  119.8 2.6 %shard_map.188 = (bf16[128,2048]{1,0:T(8,128)(2,1)}, bf16[128,2048]{1,0:T(8,128)(2,1)}) custom-call(bf16[128,2048]{1,0:T(8,128)(2,1)} %get-tuple-element.63.right, bf16[128,2048]{1,0:T(8,128)(2,1)} %get-tuple-element.64.left, bf16[128,2048]{1,0:T(8,128)(2,1)} %collective-permute-done.21.up, bf16[128,2048]{1,0:T(8,128)(2,1)} %collective-permute-done.22.down), custom_call_target="tpu_custom_call" | custom-call | tf_op jit(solution)/shard_map/pallas_call | solution.py:313
  122.5 1.6 fusion.6
  124.9 2.7 %shard_map.190 = (bf16[144,2048]{1,0:T(8,128)(2,1)}, bf16[128,2048]{1,0:T(8,128)(2,1)}) custom-call(bf16[128,2048]{1,0:T(8,128)(2,1)} %get-tuple-element.72.right, bf16[128,2048]{1,0:T(8,128)(2,1)} %get-tuple-element.73.left, bf16[144,2048]{1,0:T(8,128)(2,1)} %copy-done.6, bf16[144,2048]{1,0:T(8,128)(2,1)} %copy-done.7), custom_call_target="tpu_custom_call" | custom-call | tf_op jit(solution)/shard_map/pallas_call | solution.py:313
  128.3 2.7 %collective-permute-start.26 = (bf16[128,2048]{1,0:T(8,128)(2,1)}, bf16[128,2048]{1,0:T(8,128)(2,1)S(1)}, u32[]{:S(2)}, u32[]{:S(2)}) collective-permute-start(bf16[128,2048]{1,0:T(8,128)(2,1)} %get-tuple-element.70), channel_id=1, source_target_pairs={{0,12},{1,49},{4,0},{5,53},{8,4},{9,57},{12,8},{13,61},{16,28},{17... | collective-permute-start | bytes 1572872 | tf_op jit(solution)/shard_map/ppermute | solution.py:37
  131.1 2.7 %collective-permute-start.31 = (bf16[128,2048]{1,0:T(8,128)(2,1)}, bf16[128,2048]{1,0:T(8,128)(2,1)}, u32[]{:S(2)}, u32[]{:S(2)}) collective-permute-start(bf16[128,2048]{1,0:T(8,128)(2,1)} %get-tuple-element.78), channel_id=1, source_target_pairs={{0,12},{1,49},{4,0},{5,53},{8,4},{9,57},{12,8},{13,61},{16,28},{17... | collective-permute-start | bytes 1572872 | tf_op jit(solution)/shard_map/ppermute | solution.py:37
  135.4 1.6 fusion.2
  138.3 3.2 %shard_map.189.video = bf16[256,2048]{1,0:T(8,128)(2,1)} custom-call(bf16[256,2048]{1,0:T(8,128)(2,1)} %get-tuple-element.62.own, bf16[128,2048]{1,0:T(8,128)(2,1)} %collective-permute-done.23.up_a, bf16[128,2048]{1,0:T(8,128)(2,1)} %collective-permute-done.24.up_b, bf16[128,2048]{1,0:T(8,128)(2,1)} %collective-permute-done.25.down_a, ...), custom_call_target="tpu_custom_call" | custom-call | tf_op jit(solution)/shard_map/pallas_call | solution.py:313
  141.5 4.8 %collective-permute-start.20 = (f32[144,1024]{1,0:T(8,128)}, f32[144,1024]{1,0:T(8,128)S(1)}, u32[]{:S(2)}, u32[]{:S(2)}) collective-permute-start(f32[144,1024]{1,0:T(8,128)} %get-tuple-element.61), channel_id=1, source_target_pairs={{0,1},{1,0},{4,5},{5,4},{8,9},{9,8},{12,13},{13,12},{16,17},{17,16... | collective-permute-start | bytes 1769480 | tf_op jit(solution)/shard_map/ppermute | solution.py:37
  146.3 2.4 %collective-permute-done.32.down_b = bf16[128,2048]{1,0:T(8,128)(2,1)} collective-permute-done((bf16[128,2048]{1,0:T(8,128)(2,1)}, bf16[128,2048]{1,0:T(8,128)(2,1)}, u32[]{:S(2)}, u32[]{:S(2)}) %collective-permute-start.32) | collective-permute-done | bytes 524320 | tf_op jit(solution)/shard_map/ppermute | solution.py:37
  149.6 4.1 %shard_map.191 = (bf16[144,2048]{1,0:T(8,128)(2,1)}, bf16[144,2048]{1,0:T(8,128)(2,1)}, bf16[144,2048]{1,0:T(8,128)(2,1)}, bf16[128,2048]{1,0:T(8,128)(2,1)}, f32[1,2048]{1,0:T(1,128)}) custom-call(bf16[256,2048]{1,0:T(8,128)(2,1)} %shard_map.189.video, bf16[256,2048]{1,0:T(8,128)(2,1)} %get-tuple-element.71.own, bf16[144,2048]{1,0:T(8,128)(2,1)} %copy-done.15, ...), custom_call_target="tpu_custom_call" | custom-call | tf_op jit(solution)/shard_map/pallas_call | solution.py:313
  154.6 1.8 collective-permute-start.34
  161.4 2.9 %collective-permute-done.33.up = bf16[144,2048]{1,0:T(8,128)(2,1)} collective-permute-done((bf16[144,2048]{1,0:T(8,128)(2,1)}, bf16[144,2048]{1,0:T(8,128)(2,1)}, u32[]{:S(2)}, u32[]{:S(2)}) %collective-permute-start.33) | collective-permute-done | bytes 589856 | tf_op jit(solution)/shard_map/ppermute | solution.py:37
  164.2 5.6 %collective-permute-done.34.down = bf16[144,2048]{1,0:T(8,128)(2,1)} collective-permute-done((bf16[144,2048]{1,0:T(8,128)(2,1)}, bf16[144,2048]{1,0:T(8,128)(2,1)}, u32[]{:S(2)}, u32[]{:S(2)}) %collective-permute-start.34) | collective-permute-done | bytes 589856 | tf_op jit(solution)/shard_map/ppermute | solution.py:37
  169.9 1.5 collective-permute-done.35.far
  171.4 2.8 %shard_map.192 = (bf16[72,2560]{1,0:T(8,128)(2,1)}, bf16[72,2560]{1,0:T(8,128)(2,1)}, f32[1,2048]{1,0:T(1,128)}) custom-call(s32[5]{0:T(128)} %stack.50.where.refs_0_, bf16[128,2048]{1,0:T(8,128)(2,1)} %get-tuple-element.81.home, f32[1,2048]{1,0:T(1,128)} %get-tuple-element.82.gain, bf16[144,2048]{1,0:T(8,128)(2,1)} %collective-permute-done.33.up, ...), custom_call_target="tpu_custom_call" | custom-call | tf_op jit(solution)/shard_map/pallas_call | solution.py:313
  175.0 1.9 collective-permute-start.37
  179.0 2.9 %collective-permute-done.36.up = bf16[72,2560]{1,0:T(8,128)(2,1)S(1)} collective-permute-done((bf16[72,2560]{1,0:T(8,128)(2,1)}, bf16[72,2560]{1,0:T(8,128)(2,1)S(1)}, u32[]{:S(2)}, u32[]{:S(2)}) %collective-permute-start.36) | collective-permute-done | bytes 368672 | tf_op jit(solution)/shard_map/ppermute | solution.py:37
  183.2 6.4 %collective-permute-done.38.far = bf16[72,2560]{1,0:T(8,128)(2,1)S(1)} collective-permute-done((bf16[72,2560]{1,0:T(8,128)(2,1)}, bf16[72,2560]{1,0:T(8,128)(2,1)S(1)}, u32[]{:S(2)}, u32[]{:S(2)}) %collective-permute-start.38) | collective-permute-done | bytes 368672 | tf_op jit(solution)/shard_map/ppermute | solution.py:37
  190.3 2.4 %shard_map.193.mine = f32[72,2560]{1,0:T(8,128)} custom-call(bf16[72,2560]{1,0:T(8,128)(2,1)} %get-tuple-element.86.same, bf16[72,2560]{1,0:T(8,128)(2,1)} %copy-done.19, bf16[72,2560]{1,0:T(8,128)(2,1)} %copy-done.20, bf16[72,2560]{1,0:T(8,128)(2,1)} %copy-done.21, f32[1,2048]{1,0:T(1,128)} %get-tuple-element.88.gain), custom_call_target="tpu_custom_call" | custom-call | tf_op jit(solution)/shard_map/pallas_call | solution.py:313
  192.7 5.5 %collective-permute-start.39 = (f32[72,2560]{1,0:T(8,128)}, f32[72,2560]{1,0:T(8,128)S(1)}, u32[]{:S(2)}, u32[]{:S(2)}) collective-permute-start(f32[72,2560]{1,0:T(8,128)} %shard_map.193.mine), channel_id=1, source_target_pairs={{0,1},{1,0},{4,5},{5,4},{8,9},{9,8},{12,13},{13,12},{16,17},{17,16... | collective-permute-start | bytes 2211848 | tf_op jit(solution)/shard_map/ppermute | solution.py:37
  198.5 1.5 fusion.20
  201.6 2.4 %shard_map.194 = (f32[32,3072]{1,0:T(8,128)}, f32[32,1024]{1,0:T(8,128)}, f32[32,3072]{1,0:T(8,128)}, f32[32,1024]{1,0:T(8,128)}, f32[1,1024]{1,0:T(1,128)}, /*index=5*/f32[1,1024]{1,0:T(1,128)}) custom-call(s32[5]{0:T(128)} %stack.50.where.refs_0_, f32[72,2560]{1,0:T(8,128)} %shard_map.193.mine, f32[72,2560]{1,0:T(8,128)} %copy-done.13), custom_call_target="tpu_custom_call" | custom-call | tf_op jit(solution)/shard_map/pallas_call | solution.py:313
  (167 shorter events, 33.0 us)
Async XLA Ops:
  7.2 77.0 %all-gather.2.cloned.1.call-start = ((), (), s32[]{:S(2)}) async-start(), calls=%async_computation | async-start | bytes 5324800 | tf_op jit(solution)/shard_map/all_gather | solution.py:523
  11.9 49.9 %copy-start.3 = (bf16[2,208,1024]{2,1,0:T(8,128)(2,1)}, bf16[2,208,1024]{2,1,0:T(8,128)(2,1)S(1)}, u32[]{:S(2)}) copy-start(bf16[2,208,1024]{2,1,0:T(8,128)(2,1)S(1)} %pad_maximum_fusion.refs_1_) | copy-start | bytes 2555908
  11.9 35.0 %collective-permute-start = (bf16[2,208,1024]{2,1,0:T(8,128)(2,1)S(1)}, bf16[2,208,1024]{2,1,0:T(8,128)(2,1)S(1)}, u32[]{:S(2)}, u32[]{:S(2)}) collective-permute-start(bf16[2,208,1024]{2,1,0:T(8,128)(2,1)S(1)} %pad_maximum_fusion.refs_1_), channel_id=1, source_target_pairs={{0,1},{1,0},{4,5},{5,4},{8,9},{9,8},{12,13},{13,12},{16,17},{17,16... | collective-permute-start | bytes 2555912 | tf_op jit(solution)/shard_map/ppermute | solution.py:37
  14.8 69.4 %copy-start.4 = (bf16[2,144,1024]{2,1,0:T(8,128)(2,1)}, bf16[2,144,1024]{2,1,0:T(8,128)(2,1)S(1)}, u32[]{:S(2)}) copy-start(bf16[2,144,1024]{2,1,0:T(8,128)(2,1)S(1)} %pad_maximum_fusion.1.refs_1_) | copy-start | bytes 1769476
  14.8 20.0 %collective-permute-start.1 = (bf16[2,144,1024]{2,1,0:T(8,128)(2,1)S(1)}, bf16[2,144,1024]{2,1,0:T(8,128)(2,1)S(1)}, u32[]{:S(2)}, u32[]{:S(2)}) collective-permute-start(bf16[2,144,1024]{2,1,0:T(8,128)(2,1)S(1)} %pad_maximum_fusion.1.refs_1_), channel_id=1, source_target_pairs={{0,1},{1,0},{4,5},{5,4},{8,9},{9,8},{12,13},{13,12},{16,17},{17,16... | collective-permute-start | bytes 1769480 | tf_op jit(solution)/shard_map/ppermute | solution.py:37
  15.0 5.2 %collective-permute-start.2 = (bf16[16,2560]{1,0:T(8,128)(2,1)S(1)}, bf16[16,2560]{1,0:T(8,128)(2,1)S(1)}, u32[]{:S(2)}, u32[]{:S(2)}) collective-permute-start(bf16[16,2560]{1,0:T(8,128)(2,1)S(1)} %copy-done.38), channel_id=1, source_target_pairs={{0,64},{1,65},{4,68},{5,69},{8,72},{9,73},{12,76},{13,77},{16,80},... | collective-permute-start | bytes 245768 | tf_op jit(solution)/shard_map/ppermute | solution.py:37
  16.4 3.8 %collective-permute-start.3 = (bf16[16,2560]{1,0:T(8,128)(2,1)S(1)}, bf16[16,2560]{1,0:T(8,128)(2,1)S(1)}, u32[]{:S(2)}, u32[]{:S(2)}) collective-permute-start(bf16[16,2560]{1,0:T(8,128)(2,1)S(1)} %copy-done.37), channel_id=1, source_target_pairs={{0,66},{1,67},{4,70},{5,71},{8,74},{9,75},{12,78},{13,79},{16,82},... | collective-permute-start | bytes 245768 | tf_op jit(solution)/shard_map/ppermute | solution.py:37
  20.3 41.5 %copy-start.11 = (bf16[2,32,2048]{2,1,0:T(8,128)(2,1)}, bf16[2,32,2048]{2,1,0:T(8,128)(2,1)S(1)}, u32[]{:S(2)}) copy-start(bf16[2,32,2048]{2,1,0:T(8,128)(2,1)S(1)} %pad_maximum_fusion.2.refs_4_) | copy-start | bytes 786436
  20.4 6.8 %collective-permute-start.4 = (bf16[2,32,2048]{2,1,0:T(8,128)(2,1)S(1)}, bf16[2,32,2048]{2,1,0:T(8,128)(2,1)S(1)}, u32[]{:S(2)}, u32[]{:S(2)}) collective-permute-start(bf16[2,32,2048]{2,1,0:T(8,128)(2,1)S(1)} %pad_maximum_fusion.2.refs_4_), channel_id=1, source_target_pairs={{0,16},{1,5},{4,20},{5,9},{8,24},{9,13},{12,28},{13,1},{16,32},{17... | collective-permute-start | bytes 786440 | tf_op jit(solution)/shard_map/ppermute | solution.py:37
  21.5 9.3 %collective-permute-start.5 = (bf16[2,32,2048]{2,1,0:T(8,128)(2,1)S(1)}, bf16[2,32,2048]{2,1,0:T(8,128)(2,1)S(1)}, u32[]{:S(2)}, u32[]{:S(2)}) collective-permute-start(bf16[2,32,2048]{2,1,0:T(8,128)(2,1)S(1)} %pad_maximum_fusion.2.refs_4_), channel_id=1, source_target_pairs={{0,48},{1,13},{4,52},{5,1},{8,56},{9,5},{12,60},{13,9},{16,0},{17,... | collective-permute-start | bytes 786440 | tf_op jit(solution)/shard_map/ppermute | solution.py:37
  23.1 9.7 %collective-permute-start.7 = (bf16[2,32,2048]{2,1,0:T(8,128)(2,1)S(1)}, bf16[2,32,2048]{2,1,0:T(8,128)(2,1)S(1)}, u32[]{:S(2)}, u32[]{:S(2)}) collective-permute-start(bf16[2,32,2048]{2,1,0:T(8,128)(2,1)S(1)} %pad_maximum_fusion.2.refs_4_), channel_id=1, source_target_pairs={{0,4},{1,17},{4,8},{5,21},{8,12},{9,25},{12,0},{13,29},{16,20},{17... | collective-permute-start | bytes 786440 | tf_op jit(solution)/shard_map/ppermute | solution.py:37
  27.2 7.1 %collective-permute-start.11 = (bf16[2,32,2048]{2,1,0:T(8,128)(2,1)S(1)}, bf16[2,32,2048]{2,1,0:T(8,128)(2,1)S(1)}, u32[]{:S(2)}, u32[]{:S(2)}) collective-permute-start(bf16[2,32,2048]{2,1,0:T(8,128)(2,1)S(1)} %pad_maximum_fusion.2.refs_4_), channel_id=1, source_target_pairs={{0,12},{1,49},{4,0},{5,53},{8,4},{9,57},{12,8},{13,61},{16,28},{17... | collective-permute-start | bytes 786440 | tf_op jit(solution)/shard_map/ppermute | solution.py:37
  30.8 6.7 %collective-permute-start.6 = (bf16[2,32,2048]{2,1,0:T(8,128)(2,1)S(1)}, bf16[2,32,2048]{2,1,0:T(8,128)(2,1)S(1)}, u32[]{:S(2)}, u32[]{:S(2)}) collective-permute-start(bf16[2,32,2048]{2,1,0:T(8,128)(2,1)S(1)} %collective-permute-done.4.refs_5_), channel_id=1, source_target_pairs={{0,16},{1,5},{4,20},{5,9},{8,24},{9,13},{12,28},{13,1},{16,32},{17... | collective-permute-start | bytes 786440 | tf_op jit(solution)/shard_map/ppermute | solution.py:37
  32.8 6.7 %collective-permute-start.8 = (bf16[2,32,2048]{2,1,0:T(8,128)(2,1)S(1)}, bf16[2,32,2048]{2,1,0:T(8,128)(2,1)S(1)}, u32[]{:S(2)}, u32[]{:S(2)}) collective-permute-start(bf16[2,32,2048]{2,1,0:T(8,128)(2,1)S(1)} %collective-permute-done.4.refs_5_), channel_id=1, source_target_pairs={{0,4},{1,17},{4,8},{5,21},{8,12},{9,25},{12,0},{13,29},{16,20},{17... | collective-permute-start | bytes 786440 | tf_op jit(solution)/shard_map/ppermute | solution.py:37
  34.3 10.7 %collective-permute-start.9 = (bf16[2,32,2048]{2,1,0:T(8,128)(2,1)S(1)}, bf16[2,32,2048]{2,1,0:T(8,128)(2,1)S(1)}, u32[]{:S(2)}, u32[]{:S(2)}) collective-permute-start(bf16[2,32,2048]{2,1,0:T(8,128)(2,1)S(1)} %collective-permute-done.5.refs_6_), channel_id=1, source_target_pairs={{0,4},{1,17},{4,8},{5,21},{8,12},{9,25},{12,0},{13,29},{16,20},{17... | collective-permute-start | bytes 786440 | tf_op jit(solution)/shard_map/ppermute | solution.py:37
  34.7 49.4 %copy-start.14 = (bf16[2,144,1024]{2,1,0:T(8,128)(2,1)}, bf16[2,144,1024]{2,1,0:T(8,128)(2,1)S(1)}, u32[]{:S(2)}) copy-start(bf16[2,144,1024]{2,1,0:T(8,128)(2,1)S(1)} %collective-permute-done.1.refs_2_) | copy-start | bytes 1769476
  34.7 10.2 %collective-permute-start.12 = (bf16[2,32,2048]{2,1,0:T(8,128)(2,1)S(1)}, bf16[2,32,2048]{2,1,0:T(8,128)(2,1)S(1)}, u32[]{:S(2)}, u32[]{:S(2)}) collective-permute-start(bf16[2,32,2048]{2,1,0:T(8,128)(2,1)S(1)} %collective-permute-done.4.refs_5_), channel_id=1, source_target_pairs={{0,12},{1,49},{4,0},{5,53},{8,4},{9,57},{12,8},{13,61},{16,28},{17... | collective-permute-start | bytes 786440 | tf_op jit(solution)/shard_map/ppermute | solution.py:37
  37.5 8.1 %collective-permute-start.13 = (bf16[2,32,2048]{2,1,0:T(8,128)(2,1)S(1)}, bf16[2,32,2048]{2,1,0:T(8,128)(2,1)S(1)}, u32[]{:S(2)}, u32[]{:S(2)}) collective-permute-start(bf16[2,32,2048]{2,1,0:T(8,128)(2,1)S(1)} %collective-permute-done.5.refs_6_), channel_id=1, source_target_pairs={{0,12},{1,49},{4,0},{5,53},{8,4},{9,57},{12,8},{13,61},{16,28},{17... | collective-permute-start | bytes 786440 | tf_op jit(solution)/shard_map/ppermute | solution.py:37
  39.5 8.8 %collective-permute-start.14 = (bf16[2,32,2048]{2,1,0:T(8,128)(2,1)S(1)}, bf16[2,32,2048]{2,1,0:T(8,128)(2,1)S(1)}, u32[]{:S(2)}, u32[]{:S(2)}) collective-permute-start(bf16[2,32,2048]{2,1,0:T(8,128)(2,1)S(1)} %collective-permute-done.6.refs_7_), channel_id=1, source_target_pairs={{0,12},{1,49},{4,0},{5,53},{8,4},{9,57},{12,8},{13,61},{16,28},{17... | collective-permute-start | bytes 786440 | tf_op jit(solution)/shard_map/ppermute | solution.py:37
  45.0 7.5 %collective-permute-start.15 = (bf16[2,32,2048]{2,1,0:T(8,128)(2,1)S(1)}, bf16[2,32,2048]{2,1,0:T(8,128)(2,1)S(1)}, u32[]{:S(2)}, u32[]{:S(2)}) collective-permute-start(bf16[2,32,2048]{2,1,0:T(8,128)(2,1)S(1)} %collective-permute-done.7.refs_8_), channel_id=1, source_target_pairs={{0,4},{1,17},{4,8},{5,21},{8,12},{9,25},{12,0},{13,29},{16,20},{17... | collective-permute-start | bytes 786440 | tf_op jit(solution)/shard_map/ppermute | solution.py:37
  45.0 11.5 %collective-permute-start.10 = (bf16[2,32,2048]{2,1,0:T(8,128)(2,1)S(1)}, bf16[2,32,2048]{2,1,0:T(8,128)(2,1)S(1)}, u32[]{:S(2)}, u32[]{:S(2)}) collective-permute-start(bf16[2,32,2048]{2,1,0:T(8,128)(2,1)S(1)} %collective-permute-done.6.refs_7_), channel_id=1, source_target_pairs={{0,4},{1,17},{4,8},{5,21},{8,12},{9,25},{12,0},{13,29},{16,20},{17... | collective-permute-start | bytes 786440 | tf_op jit(solution)/shard_map/ppermute | solution.py:37
  45.6 14.8 %collective-permute-start.16 = (bf16[2,32,2048]{2,1,0:T(8,128)(2,1)S(1)}, bf16[2,32,2048]{2,1,0:T(8,128)(2,1)S(1)}, u32[]{:S(2)}, u32[]{:S(2)}) collective-permute-start(bf16[2,32,2048]{2,1,0:T(8,128)(2,1)S(1)} %collective-permute-done.8.refs_9_), channel_id=1, source_target_pairs={{0,4},{1,17},{4,8},{5,21},{8,12},{9,25},{12,0},{13,29},{16,20},{17... | collective-permute-start | bytes 786440 | tf_op jit(solution)/shard_map/ppermute | solution.py:37
  46.9 13.4 %collective-permute-start.17 = (bf16[2,32,2048]{2,1,0:T(8,128)(2,1)S(1)}, bf16[2,32,2048]{2,1,0:T(8,128)(2,1)S(1)}, u32[]{:S(2)}, u32[]{:S(2)}) collective-permute-start(bf16[2,32,2048]{2,1,0:T(8,128)(2,1)S(1)} %collective-permute-done.13.refs_14_), channel_id=1, source_target_pairs={{0,12},{1,49},{4,0},{5,53},{8,4},{9,57},{12,8},{13,61},{16,28},{17... | collective-permute-start | bytes 786440 | tf_op jit(solution)/shard_map/ppermute | solution.py:37
  48.3 12.0 %collective-permute-start.18 = (bf16[2,32,2048]{2,1,0:T(8,128)(2,1)S(1)}, bf16[2,32,2048]{2,1,0:T(8,128)(2,1)S(1)}, u32[]{:S(2)}, u32[]{:S(2)}) collective-permute-start(bf16[2,32,2048]{2,1,0:T(8,128)(2,1)S(1)} %collective-permute-done.14.refs_15_), channel_id=1, source_target_pairs={{0,12},{1,49},{4,0},{5,53},{8,4},{9,57},{12,8},{13,61},{16,28},{17... | collective-permute-start | bytes 786440 | tf_op jit(solution)/shard_map/ppermute | solution.py:37
  79.2 43.3 %copy-start = (bf16[1,196,1024]{2,1,0:T(8,128)(2,1)S(1)}, bf16[1,196,1024]{2,1,0:T(8,128)(2,1)}, u32[]{:S(2)}) copy-start(bf16[1,196,1024]{2,1,0:T(8,128)(2,1)} %param.12) | copy-start | bytes 1204228
  84.1 49.8 %copy-start.1 = (bf16[1,128,1024]{2,1,0:T(8,128)(2,1)S(1)}, bf16[1,128,1024]{2,1,0:T(8,128)(2,1)}, u32[]{:S(2)}) copy-start(bf16[1,128,1024]{2,1,0:T(8,128)(2,1)} %param.13) | copy-start | bytes 786436
  84.1 51.3 %copy-start.2 = (f32[208,1024]{1,0:T(8,128)S(1)}, f32[208,1024]{1,0:T(8,128)}, u32[]{:S(2)}) copy-start(f32[208,1024]{1,0:T(8,128)} %get-tuple-element.55) | copy-start | bytes 2555908
  101.0 21.5 %collective-permute-start.27 = (bf16[144,2048]{1,0:T(8,128)(2,1)}, bf16[144,2048]{1,0:T(8,128)(2,1)S(1)}, u32[]{:S(2)}, u32[]{:S(2)}) collective-permute-start(bf16[144,2048]{1,0:T(8,128)(2,1)} %get-tuple-element.74), channel_id=1, source_target_pairs={{0,4},{1,17},{4,8},{5,21},{8,12},{9,25},{12,0},{13,29},{16,20},{17... | collective-permute-start | bytes 1769480 | tf_op jit(solution)/shard_map/ppermute | solution.py:37
  101.9 15.2 %collective-permute-start.21 = (bf16[128,2048]{1,0:T(8,128)(2,1)}, bf16[128,2048]{1,0:T(8,128)(2,1)}, u32[]{:S(2)}, u32[]{:S(2)}) collective-permute-start(bf16[128,2048]{1,0:T(8,128)(2,1)} %get-tuple-element.65), channel_id=1, source_target_pairs={{0,4},{1,17},{4,8},{5,21},{8,12},{9,25},{12,0},{13,29},{16,20},{17... | collective-permute-start | bytes 1572872 | tf_op jit(solution)/shard_map/ppermute | solution.py:37
  103.2 13.9 %collective-permute-start.22 = (bf16[128,2048]{1,0:T(8,128)(2,1)}, bf16[128,2048]{1,0:T(8,128)(2,1)}, u32[]{:S(2)}, u32[]{:S(2)}) collective-permute-start(bf16[128,2048]{1,0:T(8,128)(2,1)} %get-tuple-element.66), channel_id=1, source_target_pairs={{0,12},{1,49},{4,0},{5,53},{8,4},{9,57},{12,8},{13,61},{16,28},{17... | collective-permute-start | bytes 1572872 | tf_op jit(solution)/shard_map/ppermute | solution.py:37
  104.6 26.4 %collective-permute-start.19 = (f32[208,1024]{1,0:T(8,128)}, f32[208,1024]{1,0:T(8,128)S(1)}, u32[]{:S(2)}, u32[]{:S(2)}) collective-permute-start(f32[208,1024]{1,0:T(8,128)} %get-tuple-element.56), channel_id=1, source_target_pairs={{0,1},{1,0},{4,5},{5,4},{8,9},{9,8},{12,13},{13,12},{16,17},{17,16... | collective-permute-start | bytes 2555912 | tf_op jit(solution)/shard_map/ppermute | solution.py:37
  106.8 17.3 %collective-permute-start.28 = (bf16[144,2048]{1,0:T(8,128)(2,1)}, bf16[144,2048]{1,0:T(8,128)(2,1)S(1)}, u32[]{:S(2)}, u32[]{:S(2)}) collective-permute-start(bf16[144,2048]{1,0:T(8,128)(2,1)} %get-tuple-element.75), channel_id=1, source_target_pairs={{0,12},{1,49},{4,0},{5,53},{8,4},{9,57},{12,8},{13,61},{16,28},{17... | collective-permute-start | bytes 1769480 | tf_op jit(solution)/shard_map/ppermute | solution.py:37
  117.1 11.2 %collective-permute-start.24 = (bf16[128,2048]{1,0:T(8,128)(2,1)}, bf16[128,2048]{1,0:T(8,128)(2,1)}, u32[]{:S(2)}, u32[]{:S(2)}) collective-permute-start(bf16[128,2048]{1,0:T(8,128)(2,1)} %get-tuple-element.68), channel_id=1, source_target_pairs={{0,4},{1,17},{4,8},{5,21},{8,12},{9,25},{12,0},{13,29},{16,20},{17... | collective-permute-start | bytes 1572872 | tf_op jit(solution)/shard_map/ppermute | solution.py:37
  117.1 13.9 %collective-permute-start.25 = (bf16[128,2048]{1,0:T(8,128)(2,1)}, bf16[128,2048]{1,0:T(8,128)(2,1)}, u32[]{:S(2)}, u32[]{:S(2)}) collective-permute-start(bf16[128,2048]{1,0:T(8,128)(2,1)} %get-tuple-element.69), channel_id=1, source_target_pairs={{0,12},{1,49},{4,0},{5,53},{8,4},{9,57},{12,8},{13,61},{16,28},{17... | collective-permute-start | bytes 1572872 | tf_op jit(solution)/shard_map/ppermute | solution.py:37
  122.4 11.3 %collective-permute-start.23 = (bf16[128,2048]{1,0:T(8,128)(2,1)}, bf16[128,2048]{1,0:T(8,128)(2,1)}, u32[]{:S(2)}, u32[]{:S(2)}) collective-permute-start(bf16[128,2048]{1,0:T(8,128)(2,1)} %get-tuple-element.67), channel_id=1, source_target_pairs={{0,4},{1,17},{4,8},{5,21},{8,12},{9,25},{12,0},{13,29},{16,20},{17... | collective-permute-start | bytes 1572872 | tf_op jit(solution)/shard_map/ppermute | solution.py:37
  127.6 21.1 %collective-permute-start.29 = (bf16[144,2048]{1,0:T(8,128)(2,1)}, bf16[144,2048]{1,0:T(8,128)(2,1)S(1)}, u32[]{:S(2)}, u32[]{:S(2)}) collective-permute-start(bf16[144,2048]{1,0:T(8,128)(2,1)} %get-tuple-element.76), channel_id=1, source_target_pairs={{0,4},{1,17},{4,8},{5,21},{8,12},{9,25},{12,0},{13,29},{16,20},{17... | collective-permute-start | bytes 1769480 | tf_op jit(solution)/shard_map/ppermute | solution.py:37
  128.3 9.2 %collective-permute-start.26 = (bf16[128,2048]{1,0:T(8,128)(2,1)}, bf16[128,2048]{1,0:T(8,128)(2,1)S(1)}, u32[]{:S(2)}, u32[]{:S(2)}) collective-permute-start(bf16[128,2048]{1,0:T(8,128)(2,1)} %get-tuple-element.70), channel_id=1, source_target_pairs={{0,12},{1,49},{4,0},{5,53},{8,4},{9,57},{12,8},{13,61},{16,28},{17... | collective-permute-start | bytes 1572872 | tf_op jit(solution)/shard_map/ppermute | solution.py:37
  131.1 15.2 %collective-permute-start.30 = (bf16[128,2048]{1,0:T(8,128)(2,1)}, bf16[128,2048]{1,0:T(8,128)(2,1)}, u32[]{:S(2)}, u32[]{:S(2)}) collective-permute-start(bf16[128,2048]{1,0:T(8,128)(2,1)} %get-tuple-element.77), channel_id=1, source_target_pairs={{0,4},{1,17},{4,8},{5,21},{8,12},{9,25},{12,0},{13,29},{16,20},{17... | collective-permute-start | bytes 1572872 | tf_op jit(solution)/shard_map/ppermute | solution.py:37
  131.1 15.2 %collective-permute-start.31 = (bf16[128,2048]{1,0:T(8,128)(2,1)}, bf16[128,2048]{1,0:T(8,128)(2,1)}, u32[]{:S(2)}, u32[]{:S(2)}) collective-permute-start(bf16[128,2048]{1,0:T(8,128)(2,1)} %get-tuple-element.78), channel_id=1, source_target_pairs={{0,12},{1,49},{4,0},{5,53},{8,4},{9,57},{12,8},{13,61},{16,28},{17... | collective-permute-start | bytes 1572872 | tf_op jit(solution)/shard_map/ppermute | solution.py:37
  133.7 15.0 %collective-permute-start.32 = (bf16[128,2048]{1,0:T(8,128)(2,1)}, bf16[128,2048]{1,0:T(8,128)(2,1)}, u32[]{:S(2)}, u32[]{:S(2)}) collective-permute-start(bf16[128,2048]{1,0:T(8,128)(2,1)} %get-tuple-element.79), channel_id=1, source_target_pairs={{0,12},{1,49},{4,0},{5,53},{8,4},{9,57},{12,8},{13,61},{16,28},{17... | collective-permute-start | bytes 1572872 | tf_op jit(solution)/shard_map/ppermute | solution.py:37
  141.5 36.5 %collective-permute-start.20 = (f32[144,1024]{1,0:T(8,128)}, f32[144,1024]{1,0:T(8,128)S(1)}, u32[]{:S(2)}, u32[]{:S(2)}) collective-permute-start(f32[144,1024]{1,0:T(8,128)} %get-tuple-element.61), channel_id=1, source_target_pairs={{0,1},{1,0},{4,5},{5,4},{8,9},{9,8},{12,13},{13,12},{16,17},{17,16... | collective-permute-start | bytes 1769480 | tf_op jit(solution)/shard_map/ppermute | solution.py:37
  153.7 10.6 %collective-permute-start.33 = (bf16[144,2048]{1,0:T(8,128)(2,1)}, bf16[144,2048]{1,0:T(8,128)(2,1)}, u32[]{:S(2)}, u32[]{:S(2)}) collective-permute-start(bf16[144,2048]{1,0:T(8,128)(2,1)} %get-tuple-element.83), channel_id=1, source_target_pairs={{0,16},{1,5},{4,20},{5,9},{8,24},{9,13},{12,28},{13,1},{16,32},{17... | collective-permute-start | bytes 1769480 | tf_op jit(solution)/shard_map/ppermute | solution.py:37
  154.6 15.3 %collective-permute-start.34 = (bf16[144,2048]{1,0:T(8,128)(2,1)}, bf16[144,2048]{1,0:T(8,128)(2,1)}, u32[]{:S(2)}, u32[]{:S(2)}) collective-permute-start(bf16[144,2048]{1,0:T(8,128)(2,1)} %get-tuple-element.84), channel_id=1, source_target_pairs={{0,48},{1,13},{4,52},{5,1},{8,56},{9,5},{12,60},{13,9},{16,0},{17,... | collective-permute-start | bytes 1769480 | tf_op jit(solution)/shard_map/ppermute | solution.py:37
  156.4 15.0 %collective-permute-start.35 = (bf16[144,2048]{1,0:T(8,128)(2,1)}, bf16[144,2048]{1,0:T(8,128)(2,1)}, u32[]{:S(2)}, u32[]{:S(2)}) collective-permute-start(bf16[144,2048]{1,0:T(8,128)(2,1)} %get-tuple-element.85), channel_id=1, source_target_pairs={{0,32},{1,9},{4,36},{5,13},{8,40},{9,1},{12,44},{13,5},{16,48},{17... | collective-permute-start | bytes 1769480 | tf_op jit(solution)/shard_map/ppermute | solution.py:37
  174.2 7.8 %collective-permute-start.36 = (bf16[72,2560]{1,0:T(8,128)(2,1)}, bf16[72,2560]{1,0:T(8,128)(2,1)S(1)}, u32[]{:S(2)}, u32[]{:S(2)}) collective-permute-start(bf16[72,2560]{1,0:T(8,128)(2,1)} %get-tuple-element.87), channel_id=1, source_target_pairs={{0,64},{1,65},{4,68},{5,69},{8,72},{9,73},{12,76},{13,77},{16,80},... | collective-permute-start | bytes 1105928 | tf_op jit(solution)/shard_map/ppermute | solution.py:37
  175.0 8.2 %collective-permute-start.37 = (bf16[72,2560]{1,0:T(8,128)(2,1)}, bf16[72,2560]{1,0:T(8,128)(2,1)S(1)}, u32[]{:S(2)}, u32[]{:S(2)}) collective-permute-start(bf16[72,2560]{1,0:T(8,128)(2,1)} %get-tuple-element.87), channel_id=1, source_target_pairs={{0,66},{1,67},{4,70},{5,71},{8,74},{9,75},{12,78},{13,79},{16,82},... | collective-permute-start | bytes 1105928 | tf_op jit(solution)/shard_map/ppermute | solution.py:37
  176.9 12.7 %collective-permute-start.38 = (bf16[72,2560]{1,0:T(8,128)(2,1)}, bf16[72,2560]{1,0:T(8,128)(2,1)S(1)}, u32[]{:S(2)}, u32[]{:S(2)}) collective-permute-start(bf16[72,2560]{1,0:T(8,128)(2,1)} %get-tuple-element.86.same), channel_id=1, source_target_pairs={{0,2},{1,3},{4,6},{5,7},{8,10},{9,11},{12,14},{13,15},{16,18},{17,... | collective-permute-start | bytes 1105928 | tf_op jit(solution)/shard_map/ppermute | solution.py:37
  192.7 8.0 %collective-permute-start.39 = (f32[72,2560]{1,0:T(8,128)}, f32[72,2560]{1,0:T(8,128)S(1)}, u32[]{:S(2)}, u32[]{:S(2)}) collective-permute-start(f32[72,2560]{1,0:T(8,128)} %shard_map.193.mine), channel_id=1, source_target_pairs={{0,1},{1,0},{4,5},{5,4},{8,9},{9,8},{12,13},{13,12},{16,17},{17,16... | collective-permute-start | bytes 2211848 | tf_op jit(solution)/shard_map/ppermute | solution.py:37
  (38 other events, 519.3 us)
Sparse Core Ops, SparseCore 0:
  10.8 73.2 all-gather.1
